TPU v7x, 16 devices: a 4x2x1 block of a 4x4x8 slice. The times are simulated.
16 devices in a mesh: dp: 2 (over y, z), stage: 8 (over x, core).
Axes of the slice: x: 4, y: 2, z: 1, core: 2. Of those that a mesh axis runs over, the one named last changes fastest.
The devices are a block of a 4x4x8 slice.
Arguments:
- tokens: int32 [16, 128], P('dp'), parts along dimension 0
- labels: int32 [16, 128], P('dp'), parts along dimension 0
- emb_table: bfloat16 [32128, 512], replicated
- w_up: bfloat16 [8, 512, 2048], P('stage')
- w_down: bfloat16 [8, 2048, 512], P('stage')
Outputs:
- output 1: float32 [2], P('dp'), parts along dimension 0
- output 2: float32 [16, 512, 2048], P(('dp', 'stage')), parts along dimension 0
- output 3: float32 [16, 2048, 512], P(('dp', 'stage')), parts along dimension 0
- output 4: float32 [64256, 512], P('dp'), parts along dimension 0
There are 2 independent parts. A program takes and returns all parts, laid end to end along the dimension named above; an argument that names none is the same for every part.
All inputs are finite; a program needn't handle non-finite values.
Results may differ from a plain program's by a relative error of at most 0.02.
Values are sent between devices in bfloat16 or wider.
A program may use at most 768 MiB of HBM per device.

v0:
```python
import jax
import jax.numpy as jnp
from jax import lax
from jax.sharding import PartitionSpec as P


def rms_normalize(x_act):
    x_wide = x_act.astype(jnp.float32)
    inv_rms = lax.rsqrt(jnp.mean(x_wide * x_wide, axis=-1, keepdims=True) + 1e-6)
    return (x_wide * inv_rms).astype(jnp.bfloat16)


def block_forward(x_act, w_up, w_down):
    pre_act = jnp.dot(x_act, w_up, preferred_element_type=jnp.float32).astype(jnp.bfloat16)
    hidden = jax.nn.gelu(pre_act.astype(jnp.float32)).astype(jnp.bfloat16)
    branch = jnp.dot(hidden, w_down, preferred_element_type=jnp.float32)
    return (x_act.astype(jnp.float32) + branch).astype(jnp.bfloat16), pre_act, hidden


def block_backward(x_act, pre_act, hidden, grad_out, w_up, w_down):
    grad_down = jnp.einsum("tf,td->fd", hidden, grad_out, preferred_element_type=jnp.float32)
    grad_hidden = jnp.einsum("td,fd->tf", grad_out, w_down, preferred_element_type=jnp.float32).astype(jnp.bfloat16)
    gelu_vjp = jax.vjp(jax.nn.gelu, pre_act.astype(jnp.float32))[1]
    grad_pre = gelu_vjp(grad_hidden.astype(jnp.float32))[0].astype(jnp.bfloat16)
    grad_up = jnp.einsum("td,tf->df", x_act, grad_pre, preferred_element_type=jnp.float32)
    back_flow = jnp.einsum("tf,df->td", grad_pre, w_up, preferred_element_type=jnp.float32)
    grad_in = (grad_out.astype(jnp.float32) + back_flow).astype(jnp.bfloat16)
    return grad_in, grad_up, grad_down


def head_step(x_act, lab_row, emb_table, grad_emb, inv_count):
    logit_scale = emb_table.shape[1] ** -0.5
    normed, norm_vjp = jax.vjp(rms_normalize, x_act)
    logits = (jnp.einsum("td,vd->tv", normed, emb_table, preferred_element_type=jnp.float32) * logit_scale).astype(jnp.bfloat16)
    logit_f = logits.astype(jnp.float32)
    row_max = jnp.max(logit_f, axis=-1, keepdims=True)
    exp_shift = jnp.exp(logit_f - row_max)
    exp_total = jnp.sum(exp_shift, axis=-1, keepdims=True)
    is_label = lax.broadcasted_iota(jnp.int32, logit_f.shape, 1) == lab_row[:, None]
    picked = jnp.sum(jnp.where(is_label, logit_f, 0.0), axis=-1)
    loss_part = jnp.sum(row_max[:, 0] + jnp.log(exp_total[:, 0]) - picked) * inv_count
    grad_logits = ((exp_shift / exp_total - is_label.astype(jnp.float32)) * inv_count).astype(jnp.bfloat16)
    grad_emb = grad_emb + jnp.einsum("tv,td->vd", grad_logits, normed, preferred_element_type=jnp.float32) * logit_scale
    grad_normed = (jnp.einsum("tv,vd->td", grad_logits, emb_table, preferred_element_type=jnp.float32) * logit_scale).astype(jnp.bfloat16)
    return norm_vjp(grad_normed)[0], grad_emb, loss_part


def solution(mesh):
    n_stage = mesh.shape["stage"]
    fwd_perm = [(stage_id, stage_id + 1) for stage_id in range(n_stage - 1)]
    bwd_perm = [(stage_id + 1, stage_id) for stage_id in range(n_stage - 1)]

    def device_fn(tokens, labels, emb_table, w_up, w_down):
        n_micro, seq_len = tokens.shape
        vocab_rows, model_dim = emb_table.shape
        w_up = w_up[0]
        w_down = w_down[0]
        ffn_dim = w_up.shape[1]
        stage_idx = lax.axis_index("stage")
        is_first = stage_idx == 0
        is_last = stage_idx == n_stage - 1
        n_slots = min(n_micro, 2 * n_stage - 1)
        n_ticks = n_micro + 2 * n_stage - 2
        inv_count = 1.0 / (n_micro * seq_len)

        def tick(tick_idx, loop_state):
            recv_act, recv_grad, stash_x, stash_pre, stash_hid, acc_up, acc_down, grad_emb, loss_acc = loop_state
            micro_f = tick_idx - stage_idx
            fwd_ok = (micro_f >= 0) & (micro_f < n_micro)
            idx_f = jnp.clip(micro_f, 0, n_micro - 1)
            slot_f = idx_f % n_slots
            micro_b = tick_idx - (2 * n_stage - 2) + stage_idx
            bwd_ok = (micro_b >= 0) & (micro_b < n_micro)
            idx_b = jnp.clip(micro_b, 0, n_micro - 1)
            slot_b = idx_b % n_slots
            tok_f = lax.dynamic_index_in_dim(tokens, idx_f, 0, keepdims=False)
            lab_f = lax.dynamic_index_in_dim(labels, idx_f, 0, keepdims=False)
            x_in = jnp.where(is_first, jnp.take(emb_table, tok_f, axis=0), recv_act)

            def run_fwd(branch_in):
                y_out, pre_act, hidden = block_forward(x_in, w_up, w_down)
                return (y_out, lax.dynamic_update_index_in_dim(branch_in[0], x_in, slot_f, 0), lax.dynamic_update_index_in_dim(branch_in[1], pre_act, slot_f, 0), lax.dynamic_update_index_in_dim(branch_in[2], hidden, slot_f, 0))

            def skip_fwd(branch_in):
                return (jnp.zeros_like(x_in),) + branch_in

            y_out, stash_x, stash_pre, stash_hid = lax.cond(fwd_ok, run_fwd, skip_fwd, (stash_x, stash_pre, stash_hid))

            def run_head(branch_in):
                grad_x, new_emb, loss_part = head_step(y_out, lab_f, emb_table, branch_in[0], inv_count)
                return grad_x, new_emb, branch_in[1] + loss_part

            def skip_head(branch_in):
                return jnp.zeros_like(y_out), branch_in[0], branch_in[1]

            head_grad, grad_emb, loss_acc = lax.cond(is_last & fwd_ok, run_head, skip_head, (grad_emb, loss_acc))
            grad_out = jnp.where(is_last, head_grad, recv_grad)

            def run_bwd(branch_in):
                x_saved = lax.dynamic_index_in_dim(stash_x, slot_b, 0, keepdims=False)
                pre_saved = lax.dynamic_index_in_dim(stash_pre, slot_b, 0, keepdims=False)
                hid_saved = lax.dynamic_index_in_dim(stash_hid, slot_b, 0, keepdims=False)
                grad_in, g_up, g_down = block_backward(x_saved, pre_saved, hid_saved, grad_out, w_up, w_down)
                return grad_in, branch_in[0] + g_up, branch_in[1] + g_down

            def skip_bwd(branch_in):
                return jnp.zeros_like(grad_out), branch_in[0], branch_in[1]

            grad_in, acc_up, acc_down = lax.cond(bwd_ok, run_bwd, skip_bwd, (acc_up, acc_down))
            tok_b = lax.dynamic_index_in_dim(tokens, idx_b, 0, keepdims=False)
            emb_rows = jnp.where(is_first, grad_in, jnp.zeros_like(grad_in)).astype(jnp.float32)
            grad_emb = grad_emb.at[tok_b].add(emb_rows)
            recv_act = lax.ppermute(y_out, "stage", fwd_perm)
            recv_grad = lax.ppermute(grad_in, "stage", bwd_perm)
            return (recv_act, recv_grad, stash_x, stash_pre, stash_hid, acc_up, acc_down, grad_emb, loss_acc)

        zeros_act = jnp.zeros((seq_len, model_dim), jnp.bfloat16)
        init_carry = (zeros_act, zeros_act, jnp.zeros((n_slots, seq_len, model_dim), jnp.bfloat16), jnp.zeros((n_slots, seq_len, ffn_dim), jnp.bfloat16), jnp.zeros((n_slots, seq_len, ffn_dim), jnp.bfloat16), jnp.zeros((model_dim, ffn_dim), jnp.float32), jnp.zeros((ffn_dim, model_dim), jnp.float32), jnp.zeros((vocab_rows, model_dim), jnp.float32), jnp.zeros((), jnp.float32))
        final_state = lax.fori_loop(0, n_ticks, tick, init_carry)
        grad_emb = lax.psum(final_state[7], "stage")
        loss_total = lax.psum(final_state[8], "stage")
        return loss_total.reshape(1), final_state[5][None], final_state[6][None], grad_emb

    return jax.shard_map(device_fn, mesh=mesh, in_specs=(P("dp", None), P("dp", None), P(None, None), P("stage", None, None), P("stage", None, None)), out_specs=(P("dp"), P(("dp", "stage"), None, None), P(("dp", "stage"), None, None), P("dp", None)), check_vma=False)
```

profile of v0, /device:TPU:125, one launch (start us, length us, event | category | flops | bytes accessed | tf_op | source)
XLA Modules:
  0.0 2223.7 jit_solution(18242321716006041663)
XLA Ops:
  12.3 21.3 broadcast_in_dim.92
  39.7 1480.8 %while.31 = (s32[]{:T(128)}, bf16[128,512]{1,0:T(8,128)(2,1)S(1)}, bf16[128,512]{1,0:T(8,128)(2,1)S(1)}, bf16[8,128,512]{2,1,0:T(8,128)(2,1)}, bf16[8,128,2048]{...) while((s32[]{:T(128)}, bf16[128,512]{1,0:T(8,128)(2,1)S(1)}, ...), condition=%wide.region_14.15_spmd, body=%wide.region_0.14_spmd.sunk | while | flops 14395362304 | bytes 333210880 | solution.py:119
  46.7 15.9 scatter_fusion
  69.8 15.9 scatter_fusion
  92.9 15.9 scatter_fusion
  116.0 15.9 scatter_fusion
  136.5 34.8 %collective-permute-start.1 = (bf16[128,512]{1,0:T(8,128)(2,1)S(1)}, bf16[128,512]{1,0:T(8,128)(2,1)S(1)}, u32[]{:S(2)}, u32[]{:S(2)}) collective-permute-start(bf16[128,512]{1,0:T(8,128)(2,1)S(1)} %get-tuple-element.1049), channel_id=1, source_target_pairs={{1,0},{2,1},{3,2},{4,3},{5,4},{6,5},{7,6},{9,8},{10,9},{11,10},{12... | collective-permute-start | bytes 393224 | tf_op jit(solution)/shard_map/while/body/eval_jaxpr/ppermute | solution.py:114
  172.0 15.9 scatter_fusion
  203.2 15.9 scatter_fusion
  234.3 15.9 scatter_fusion
  265.5 15.9 scatter_fusion
  290.1 87.5 %collective-permute-start = (bf16[128,512]{1,0:T(8,128)(2,1)}, bf16[128,512]{1,0:T(8,128)(2,1)S(1)}, u32[]{:S(2)}, u32[]{:S(2)}) collective-permute-start(bf16[128,512]{1,0:T(8,128)(2,1)} %get-tuple-element.1044), channel_id=1, source_target_pairs={{0,1},{1,2},{2,3},{3,4},{4,5},{5,6},{6,7},{8,9},{9,10},{10,11},{11... | collective-permute-start | bytes 393224 | tf_op jit(solution)/shard_map/while/body/eval_jaxpr/ppermute | solution.py:113
  380.4 15.9 scatter_fusion
  396.3 11.8 collective-permute-done.1
  416.9 94.4 %collective-permute-start = (bf16[128,512]{1,0:T(8,128)(2,1)}, bf16[128,512]{1,0:T(8,128)(2,1)S(1)}, u32[]{:S(2)}, u32[]{:S(2)}) collective-permute-start(bf16[128,512]{1,0:T(8,128)(2,1)} %get-tuple-element.1044), channel_id=1, source_target_pairs={{0,1},{1,2},{2,3},{3,4},{4,5},{5,6},{6,7},{8,9},{9,10},{10,11},{11... | collective-permute-start | bytes 393224 | tf_op jit(solution)/shard_map/while/body/eval_jaxpr/ppermute | solution.py:113
  511.4 10.1 conditional.8
  524.1 15.9 scatter_fusion
  550.5 94.4 %collective-permute-start = (bf16[128,512]{1,0:T(8,128)(2,1)}, bf16[128,512]{1,0:T(8,128)(2,1)S(1)}, u32[]{:S(2)}, u32[]{:S(2)}) collective-permute-start(bf16[128,512]{1,0:T(8,128)(2,1)} %get-tuple-element.1044), channel_id=1, source_target_pairs={{0,1},{1,2},{2,3},{3,4},{4,5},{5,6},{6,7},{8,9},{9,10},{10,11},{11... | collective-permute-start | bytes 393224 | tf_op jit(solution)/shard_map/while/body/eval_jaxpr/ppermute | solution.py:113
  645.0 10.0 conditional.8
  657.7 15.9 scatter_fusion
  684.2 94.4 %collective-permute-start = (bf16[128,512]{1,0:T(8,128)(2,1)}, bf16[128,512]{1,0:T(8,128)(2,1)S(1)}, u32[]{:S(2)}, u32[]{:S(2)}) collective-permute-start(bf16[128,512]{1,0:T(8,128)(2,1)} %get-tuple-element.1044), channel_id=1, source_target_pairs={{0,1},{1,2},{2,3},{3,4},{4,5},{5,6},{6,7},{8,9},{9,10},{10,11},{11... | collective-permute-start | bytes 393224 | tf_op jit(solution)/shard_map/while/body/eval_jaxpr/ppermute | solution.py:113
  778.6 10.0 conditional.8
  791.4 15.9 scatter_fusion
  817.9 94.4 %collective-permute-start = (bf16[128,512]{1,0:T(8,128)(2,1)}, bf16[128,512]{1,0:T(8,128)(2,1)S(1)}, u32[]{:S(2)}, u32[]{:S(2)}) collective-permute-start(bf16[128,512]{1,0:T(8,128)(2,1)} %get-tuple-element.1044), channel_id=1, source_target_pairs={{0,1},{1,2},{2,3},{3,4},{4,5},{5,6},{6,7},{8,9},{9,10},{10,11},{11... | collective-permute-start | bytes 393224 | tf_op jit(solution)/shard_map/while/body/eval_jaxpr/ppermute | solution.py:113
  912.3 10.0 conditional.8
  925.0 15.9 scatter_fusion
  943.5 102.4 %collective-permute-start = (bf16[128,512]{1,0:T(8,128)(2,1)}, bf16[128,512]{1,0:T(8,128)(2,1)S(1)}, u32[]{:S(2)}, u32[]{:S(2)}) collective-permute-start(bf16[128,512]{1,0:T(8,128)(2,1)} %get-tuple-element.1044), channel_id=1, source_target_pairs={{0,1},{1,2},{2,3},{3,4},{4,5},{5,6},{6,7},{8,9},{9,10},{10,11},{11... | collective-permute-start | bytes 393224 | tf_op jit(solution)/shard_map/while/body/eval_jaxpr/ppermute | solution.py:113
  1058.7 15.9 scatter_fusion
  1077.1 94.4 %collective-permute-start = (bf16[128,512]{1,0:T(8,128)(2,1)}, bf16[128,512]{1,0:T(8,128)(2,1)S(1)}, u32[]{:S(2)}, u32[]{:S(2)}) collective-permute-start(bf16[128,512]{1,0:T(8,128)(2,1)} %get-tuple-element.1044), channel_id=1, source_target_pairs={{0,1},{1,2},{2,3},{3,4},{4,5},{5,6},{6,7},{8,9},{9,10},{10,11},{11... | collective-permute-start | bytes 393224 | tf_op jit(solution)/shard_map/while/body/eval_jaxpr/ppermute | solution.py:113
  1171.6 10.0 conditional.8
  1184.3 15.9 scatter_fusion
  1210.8 94.4 %collective-permute-start = (bf16[128,512]{1,0:T(8,128)(2,1)}, bf16[128,512]{1,0:T(8,128)(2,1)S(1)}, u32[]{:S(2)}, u32[]{:S(2)}) collective-permute-start(bf16[128,512]{1,0:T(8,128)(2,1)} %get-tuple-element.1044), channel_id=1, source_target_pairs={{0,1},{1,2},{2,3},{3,4},{4,5},{5,6},{6,7},{8,9},{9,10},{10,11},{11... | collective-permute-start | bytes 393224 | tf_op jit(solution)/shard_map/while/body/eval_jaxpr/ppermute | solution.py:113
  1305.2 10.0 conditional.8
  1317.9 15.9 scatter_fusion
  1336.4 15.9 collective-permute-start
  1352.4 10.0 conditional.8
  1365.1 15.9 scatter_fusion
  1385.5 10.7 collective-permute-start.1
  1397.0 15.9 scatter_fusion
  1418.8 15.9 scatter_fusion
  1438.8 11.9 collective-permute-start.1
  1451.4 15.9 scatter_fusion
  1474.5 15.9 scatter_fusion
  1493.2 10.7 collective-permute-start.1
  1504.7 15.9 scatter_fusion
  1520.6 29.8 %psum.14 = f32[1]{0:T(128)} all-reduce(f32[1]{0:T(128)} %bitcast.15), channel_id=1, replica_groups=mesh['dp'=2,'stage'=8] {'stage'}, use_global_device_ids=true, to_apply=%region_15.16 | all-reduce | flops 1 | bytes 8 | tf_op jit(solution)/shard_map/psum | solution.py:121
  1550.5 623.2 %all-reduce.2.cloned.1.call-done = f32[32128,512]{1,0:T(8,128)} async-done(((f32[32128,512]{1,0:T(8,128)}), f32[32128,512]{1,0:T(8,128)}) %all-reduce.2.cloned.1.call-update) | async-done | bytes 65798160 | tf_op jit(solution)/shard_map/psum | solution.py:120
  2173.7 43.1 %copy.66 = f32[32128,512]{1,0:T(8,128)} copy(f32[32128,512]{1,0:T(8,128)} %all-reduce.2.cloned.1.call-done) | data formatting | bytes 131596288
  (464 shorter events, 377.0 us)
Async XLA Ops:
  7.2 2166.5 %all-reduce.2.cloned.1.call-start = ((), (), s32[]{:S(2)}) async-start(), calls=%async_computation | async-start | bytes 131596288 | tf_op jit(solution)/shard_map/psum | solution.py:120
  33.6 6.1 copy-start.4
  40.4 22.2 collective-permute-start
  44.0 18.6 collective-permute-start.1
  63.4 22.4 %collective-permute-start = (bf16[128,512]{1,0:T(8,128)(2,1)}, bf16[128,512]{1,0:T(8,128)(2,1)S(1)}, u32[]{:S(2)}, u32[]{:S(2)}) collective-permute-start(bf16[128,512]{1,0:T(8,128)(2,1)} %get-tuple-element.1044), channel_id=1, source_target_pairs={{0,1},{1,2},{2,3},{3,4},{4,5},{5,6},{6,7},{8,9},{9,10},{10,11},{11... | collective-permute-start | bytes 393224 | tf_op jit(solution)/shard_map/while/body/eval_jaxpr/ppermute | solution.py:113
  67.1 18.6 collective-permute-start.1
  86.5 22.4 %collective-permute-start = (bf16[128,512]{1,0:T(8,128)(2,1)}, bf16[128,512]{1,0:T(8,128)(2,1)S(1)}, u32[]{:S(2)}, u32[]{:S(2)}) collective-permute-start(bf16[128,512]{1,0:T(8,128)(2,1)} %get-tuple-element.1044), channel_id=1, source_target_pairs={{0,1},{1,2},{2,3},{3,4},{4,5},{5,6},{6,7},{8,9},{9,10},{10,11},{11... | collective-permute-start | bytes 393224 | tf_op jit(solution)/shard_map/while/body/eval_jaxpr/ppermute | solution.py:113
  90.3 18.6 collective-permute-start.1
  109.6 22.4 %collective-permute-start = (bf16[128,512]{1,0:T(8,128)(2,1)}, bf16[128,512]{1,0:T(8,128)(2,1)S(1)}, u32[]{:S(2)}, u32[]{:S(2)}) collective-permute-start(bf16[128,512]{1,0:T(8,128)(2,1)} %get-tuple-element.1044), channel_id=1, source_target_pairs={{0,1},{1,2},{2,3},{3,4},{4,5},{5,6},{6,7},{8,9},{9,10},{10,11},{11... | collective-permute-start | bytes 393224 | tf_op jit(solution)/shard_map/while/body/eval_jaxpr/ppermute | solution.py:113
  113.4 18.6 collective-permute-start.1
  132.7 55.2 %collective-permute-start = (bf16[128,512]{1,0:T(8,128)(2,1)}, bf16[128,512]{1,0:T(8,128)(2,1)S(1)}, u32[]{:S(2)}, u32[]{:S(2)}) collective-permute-start(bf16[128,512]{1,0:T(8,128)(2,1)} %get-tuple-element.1044), channel_id=1, source_target_pairs={{0,1},{1,2},{2,3},{3,4},{4,5},{5,6},{6,7},{8,9},{9,10},{10,11},{11... | collective-permute-start | bytes 393224 | tf_op jit(solution)/shard_map/while/body/eval_jaxpr/ppermute | solution.py:113
  136.5 51.5 %collective-permute-start.1 = (bf16[128,512]{1,0:T(8,128)(2,1)S(1)}, bf16[128,512]{1,0:T(8,128)(2,1)S(1)}, u32[]{:S(2)}, u32[]{:S(2)}) collective-permute-start(bf16[128,512]{1,0:T(8,128)(2,1)S(1)} %get-tuple-element.1049), channel_id=1, source_target_pairs={{1,0},{2,1},{3,2},{4,3},{5,4},{6,5},{7,6},{9,8},{10,9},{11,10},{12... | collective-permute-start | bytes 393224 | tf_op jit(solution)/shard_map/while/body/eval_jaxpr/ppermute | solution.py:114
  196.7 22.4 %collective-permute-start = (bf16[128,512]{1,0:T(8,128)(2,1)}, bf16[128,512]{1,0:T(8,128)(2,1)S(1)}, u32[]{:S(2)}, u32[]{:S(2)}) collective-permute-start(bf16[128,512]{1,0:T(8,128)(2,1)} %get-tuple-element.1044), channel_id=1, source_target_pairs={{0,1},{1,2},{2,3},{3,4},{4,5},{5,6},{6,7},{8,9},{9,10},{10,11},{11... | collective-permute-start | bytes 393224 | tf_op jit(solution)/shard_map/while/body/eval_jaxpr/ppermute | solution.py:113
  198.8 20.3 collective-permute-start.1
  227.9 22.3 %collective-permute-start = (bf16[128,512]{1,0:T(8,128)(2,1)}, bf16[128,512]{1,0:T(8,128)(2,1)S(1)}, u32[]{:S(2)}, u32[]{:S(2)}) collective-permute-start(bf16[128,512]{1,0:T(8,128)(2,1)} %get-tuple-element.1044), channel_id=1, source_target_pairs={{0,1},{1,2},{2,3},{3,4},{4,5},{5,6},{6,7},{8,9},{9,10},{10,11},{11... | collective-permute-start | bytes 393224 | tf_op jit(solution)/shard_map/while/body/eval_jaxpr/ppermute | solution.py:113
  230.0 20.3 collective-permute-start.1
  259.0 22.4 %collective-permute-start = (bf16[128,512]{1,0:T(8,128)(2,1)}, bf16[128,512]{1,0:T(8,128)(2,1)S(1)}, u32[]{:S(2)}, u32[]{:S(2)}) collective-permute-start(bf16[128,512]{1,0:T(8,128)(2,1)} %get-tuple-element.1044), channel_id=1, source_target_pairs={{0,1},{1,2},{2,3},{3,4},{4,5},{5,6},{6,7},{8,9},{9,10},{10,11},{11... | collective-permute-start | bytes 393224 | tf_op jit(solution)/shard_map/while/body/eval_jaxpr/ppermute | solution.py:113
  261.1 20.2 collective-permute-start.1
  290.1 106.2 %collective-permute-start = (bf16[128,512]{1,0:T(8,128)(2,1)}, bf16[128,512]{1,0:T(8,128)(2,1)S(1)}, u32[]{:S(2)}, u32[]{:S(2)}) collective-permute-start(bf16[128,512]{1,0:T(8,128)(2,1)} %get-tuple-element.1044), channel_id=1, source_target_pairs={{0,1},{1,2},{2,3},{3,4},{4,5},{5,6},{6,7},{8,9},{9,10},{10,11},{11... | collective-permute-start | bytes 393224 | tf_op jit(solution)/shard_map/while/body/eval_jaxpr/ppermute | solution.py:113
  377.7 30.4 %collective-permute-start.1 = (bf16[128,512]{1,0:T(8,128)(2,1)S(1)}, bf16[128,512]{1,0:T(8,128)(2,1)S(1)}, u32[]{:S(2)}, u32[]{:S(2)}) collective-permute-start(bf16[128,512]{1,0:T(8,128)(2,1)S(1)} %get-tuple-element.1049), channel_id=1, source_target_pairs={{1,0},{2,1},{3,2},{4,3},{5,4},{6,5},{7,6},{9,8},{10,9},{11,10},{12... | collective-permute-start | bytes 393224 | tf_op jit(solution)/shard_map/while/body/eval_jaxpr/ppermute | solution.py:114
  416.9 123.1 %collective-permute-start = (bf16[128,512]{1,0:T(8,128)(2,1)}, bf16[128,512]{1,0:T(8,128)(2,1)S(1)}, u32[]{:S(2)}, u32[]{:S(2)}) collective-permute-start(bf16[128,512]{1,0:T(8,128)(2,1)} %get-tuple-element.1044), channel_id=1, source_target_pairs={{0,1},{1,2},{2,3},{3,4},{4,5},{5,6},{6,7},{8,9},{9,10},{10,11},{11... | collective-permute-start | bytes 393224 | tf_op jit(solution)/shard_map/while/body/eval_jaxpr/ppermute | solution.py:113
  511.4 5.9 copy-start.2
  521.4 20.4 collective-permute-start.1
  550.5 123.1 %collective-permute-start = (bf16[128,512]{1,0:T(8,128)(2,1)}, bf16[128,512]{1,0:T(8,128)(2,1)S(1)}, u32[]{:S(2)}, u32[]{:S(2)}) collective-permute-start(bf16[128,512]{1,0:T(8,128)(2,1)} %get-tuple-element.1044), channel_id=1, source_target_pairs={{0,1},{1,2},{2,3},{3,4},{4,5},{5,6},{6,7},{8,9},{9,10},{10,11},{11... | collective-permute-start | bytes 393224 | tf_op jit(solution)/shard_map/while/body/eval_jaxpr/ppermute | solution.py:113
  655.1 20.4 collective-permute-start.1
  684.2 123.1 %collective-permute-start = (bf16[128,512]{1,0:T(8,128)(2,1)}, bf16[128,512]{1,0:T(8,128)(2,1)S(1)}, u32[]{:S(2)}, u32[]{:S(2)}) collective-permute-start(bf16[128,512]{1,0:T(8,128)(2,1)} %get-tuple-element.1044), channel_id=1, source_target_pairs={{0,1},{1,2},{2,3},{3,4},{4,5},{5,6},{6,7},{8,9},{9,10},{10,11},{11... | collective-permute-start | bytes 393224 | tf_op jit(solution)/shard_map/while/body/eval_jaxpr/ppermute | solution.py:113
  788.7 20.4 collective-permute-start.1
  817.9 123.1 %collective-permute-start = (bf16[128,512]{1,0:T(8,128)(2,1)}, bf16[128,512]{1,0:T(8,128)(2,1)S(1)}, u32[]{:S(2)}, u32[]{:S(2)}) collective-permute-start(bf16[128,512]{1,0:T(8,128)(2,1)} %get-tuple-element.1044), channel_id=1, source_target_pairs={{0,1},{1,2},{2,3},{3,4},{4,5},{5,6},{6,7},{8,9},{9,10},{10,11},{11... | collective-permute-start | bytes 393224 | tf_op jit(solution)/shard_map/while/body/eval_jaxpr/ppermute | solution.py:113
  922.3 20.4 collective-permute-start.1
  943.5 131.1 %collective-permute-start = (bf16[128,512]{1,0:T(8,128)(2,1)}, bf16[128,512]{1,0:T(8,128)(2,1)S(1)}, u32[]{:S(2)}, u32[]{:S(2)}) collective-permute-start(bf16[128,512]{1,0:T(8,128)(2,1)} %get-tuple-element.1044), channel_id=1, source_target_pairs={{0,1},{1,2},{2,3},{3,4},{4,5},{5,6},{6,7},{8,9},{9,10},{10,11},{11... | collective-permute-start | bytes 393224 | tf_op jit(solution)/shard_map/while/body/eval_jaxpr/ppermute | solution.py:113
  1056.0 20.4 collective-permute-start.1
  1077.1 123.1 %collective-permute-start = (bf16[128,512]{1,0:T(8,128)(2,1)}, bf16[128,512]{1,0:T(8,128)(2,1)S(1)}, u32[]{:S(2)}, u32[]{:S(2)}) collective-permute-start(bf16[128,512]{1,0:T(8,128)(2,1)} %get-tuple-element.1044), channel_id=1, source_target_pairs={{0,1},{1,2},{2,3},{3,4},{4,5},{5,6},{6,7},{8,9},{9,10},{10,11},{11... | collective-permute-start | bytes 393224 | tf_op jit(solution)/shard_map/while/body/eval_jaxpr/ppermute | solution.py:113
  1171.6 5.9 copy-start.2
  1181.6 28.4 %collective-permute-start.1 = (bf16[128,512]{1,0:T(8,128)(2,1)S(1)}, bf16[128,512]{1,0:T(8,128)(2,1)S(1)}, u32[]{:S(2)}, u32[]{:S(2)}) collective-permute-start(bf16[128,512]{1,0:T(8,128)(2,1)S(1)} %get-tuple-element.1049), channel_id=1, source_target_pairs={{1,0},{2,1},{3,2},{4,3},{5,4},{6,5},{7,6},{9,8},{10,9},{11,10},{12... | collective-permute-start | bytes 393224 | tf_op jit(solution)/shard_map/while/body/eval_jaxpr/ppermute | solution.py:114
  1210.8 123.1 %collective-permute-start = (bf16[128,512]{1,0:T(8,128)(2,1)}, bf16[128,512]{1,0:T(8,128)(2,1)S(1)}, u32[]{:S(2)}, u32[]{:S(2)}) collective-permute-start(bf16[128,512]{1,0:T(8,128)(2,1)} %get-tuple-element.1044), channel_id=1, source_target_pairs={{0,1},{1,2},{2,3},{3,4},{4,5},{5,6},{6,7},{8,9},{9,10},{10,11},{11... | collective-permute-start | bytes 393224 | tf_op jit(solution)/shard_map/while/body/eval_jaxpr/ppermute | solution.py:113
  1315.3 20.4 collective-permute-start.1
  1336.4 44.6 %collective-permute-start = (bf16[128,512]{1,0:T(8,128)(2,1)}, bf16[128,512]{1,0:T(8,128)(2,1)S(1)}, u32[]{:S(2)}, u32[]{:S(2)}) collective-permute-start(bf16[128,512]{1,0:T(8,128)(2,1)} %get-tuple-element.1044), channel_id=1, source_target_pairs={{0,1},{1,2},{2,3},{3,4},{4,5},{5,6},{6,7},{8,9},{9,10},{10,11},{11... | collective-permute-start | bytes 393224 | tf_op jit(solution)/shard_map/while/body/eval_jaxpr/ppermute | solution.py:113
  1362.4 18.6 collective-permute-start.1
  1381.7 31.1 %collective-permute-start = (bf16[128,512]{1,0:T(8,128)(2,1)}, bf16[128,512]{1,0:T(8,128)(2,1)S(1)}, u32[]{:S(2)}, u32[]{:S(2)}) collective-permute-start(bf16[128,512]{1,0:T(8,128)(2,1)} %get-tuple-element.1044), channel_id=1, source_target_pairs={{0,1},{1,2},{2,3},{3,4},{4,5},{5,6},{6,7},{8,9},{9,10},{10,11},{11... | collective-permute-start | bytes 393224 | tf_op jit(solution)/shard_map/while/body/eval_jaxpr/ppermute | solution.py:113
  1385.5 27.3 %collective-permute-start.1 = (bf16[128,512]{1,0:T(8,128)(2,1)S(1)}, bf16[128,512]{1,0:T(8,128)(2,1)S(1)}, u32[]{:S(2)}, u32[]{:S(2)}) collective-permute-start(bf16[128,512]{1,0:T(8,128)(2,1)S(1)} %get-tuple-element.1049), channel_id=1, source_target_pairs={{1,0},{2,1},{3,2},{4,3},{5,4},{6,5},{7,6},{9,8},{10,9},{11,10},{12... | collective-permute-start | bytes 393224 | tf_op jit(solution)/shard_map/while/body/eval_jaxpr/ppermute | solution.py:114
  1413.6 21.1 collective-permute-start
  1415.7 19.1 collective-permute-start.1
  1435.5 31.9 %collective-permute-start = (bf16[128,512]{1,0:T(8,128)(2,1)}, bf16[128,512]{1,0:T(8,128)(2,1)S(1)}, u32[]{:S(2)}, u32[]{:S(2)}) collective-permute-start(bf16[128,512]{1,0:T(8,128)(2,1)} %get-tuple-element.1044), channel_id=1, source_target_pairs={{0,1},{1,2},{2,3},{3,4},{4,5},{5,6},{6,7},{8,9},{9,10},{10,11},{11... | collective-permute-start | bytes 393224 | tf_op jit(solution)/shard_map/while/body/eval_jaxpr/ppermute | solution.py:113
  1438.8 28.6 %collective-permute-start.1 = (bf16[128,512]{1,0:T(8,128)(2,1)S(1)}, bf16[128,512]{1,0:T(8,128)(2,1)S(1)}, u32[]{:S(2)}, u32[]{:S(2)}) collective-permute-start(bf16[128,512]{1,0:T(8,128)(2,1)S(1)} %get-tuple-element.1049), channel_id=1, source_target_pairs={{1,0},{2,1},{3,2},{4,3},{5,4},{6,5},{7,6},{9,8},{10,9},{11,10},{12... | collective-permute-start | bytes 393224 | tf_op jit(solution)/shard_map/while/body/eval_jaxpr/ppermute | solution.py:114
  1468.1 22.4 %collective-permute-start = (bf16[128,512]{1,0:T(8,128)(2,1)}, bf16[128,512]{1,0:T(8,128)(2,1)S(1)}, u32[]{:S(2)}, u32[]{:S(2)}) collective-permute-start(bf16[128,512]{1,0:T(8,128)(2,1)} %get-tuple-element.1044), channel_id=1, source_target_pairs={{0,1},{1,2},{2,3},{3,4},{4,5},{5,6},{6,7},{8,9},{9,10},{10,11},{11... | collective-permute-start | bytes 393224 | tf_op jit(solution)/shard_map/while/body/eval_jaxpr/ppermute | solution.py:113
  1470.1 20.3 collective-permute-start.1
  1491.2 29.4 %collective-permute-start = (bf16[128,512]{1,0:T(8,128)(2,1)}, bf16[128,512]{1,0:T(8,128)(2,1)S(1)}, u32[]{:S(2)}, u32[]{:S(2)}) collective-permute-start(bf16[128,512]{1,0:T(8,128)(2,1)} %get-tuple-element.1044), channel_id=1, source_target_pairs={{0,1},{1,2},{2,3},{3,4},{4,5},{5,6},{6,7},{8,9},{9,10},{10,11},{11... | collective-permute-start | bytes 393224 | tf_op jit(solution)/shard_map/while/body/eval_jaxpr/ppermute | solution.py:113
  1493.2 27.3 %collective-permute-start.1 = (bf16[128,512]{1,0:T(8,128)(2,1)S(1)}, bf16[128,512]{1,0:T(8,128)(2,1)S(1)}, u32[]{:S(2)}, u32[]{:S(2)}) collective-permute-start(bf16[128,512]{1,0:T(8,128)(2,1)S(1)} %get-tuple-element.1049), channel_id=1, source_target_pairs={{1,0},{2,1},{3,2},{4,3},{5,4},{6,5},{7,6},{9,8},{10,9},{11,10},{12... | collective-permute-start | bytes 393224 | tf_op jit(solution)/shard_map/while/body/eval_jaxpr/ppermute | solution.py:114
  (30 other events, 98.5 us)
Sparse Core Ops, SparseCore 0:
  1520.7 652.9 all-reduce.1
where the time goes:
time: 2250 us; the launch traced here: 2220 us
  starting transfers between devices  919 us (41%)
  waiting for transfers between devices  656 us (29%)
  other arithmetic  383 us (17%)
  local copies, waits for them, and re-layouts  119 us (5%)
  matrix products  98.3 us (4%)
  blocking collectives  29.8 us (1%)
    ppermute x22, starting transfers between devices, tick(): recv_act = lax.ppermute(y_out, 'stage', fwd_perm)  809 us
    psum x1, waiting for transfers between devices, device_fn(): grad_emb = lax.psum(final_state[7], 'stage')  623 us
    scatter-add x22, other arithmetic, tick(): grad_emb = grad_emb.at[tok_b].add(emb_rows)  350 us
    ppermute x22, starting transfers between devices, tick(): recv_grad = lax.ppermute(grad_in, 'stage', bwd_perm)  110 us
  transfers between devices with their start and end apart: 45, of which 9 were waited for; matrix products, arithmetic and copies ran while one was open for 19% of the time, Pallas kernels for 0%

commit v1 on v0

v1 whole, which is shorter than its diff:
```python
import functools
import math

import jax
import jax.numpy as jnp
from jax import lax
from jax.experimental import pallas as pl
from jax.experimental.pallas import tpu as pltpu
from jax.sharding import PartitionSpec as P

MESH = pl.DeviceIdType.MESH
LOG2E = math.log2(math.e)
LN2 = math.log(2.0)
GELU_C = math.sqrt(2.0 / math.pi)
GELU_K = 0.044715
EPS = 1e-6
LANES = 128
F32 = jnp.float32
BF16 = jnp.bfloat16


def gelu_fwd(a):
    return 0.5 * a * (1.0 + jnp.tanh(GELU_C * (a + GELU_K * (a * a * a))))


def gelu_slope(a):
    a2 = a * a
    t = jnp.tanh(GELU_C * (a + GELU_K * (a2 * a)))
    return 0.5 * (1.0 + t) + (0.5 * a) * (1.0 - t * t) * (GELU_C + (3.0 * GELU_C * GELU_K) * a2)


def dot(x, y):
    return jnp.dot(x, y, preferred_element_type=F32)


def dot_t(x, y):
    return lax.dot_general(x, y, (((0,), (0,)), ((), ())), preferred_element_type=F32)


def remote(src, dst, send_sem, recv_sem, dev):
    return pltpu.make_async_remote_copy(src_ref=src, dst_ref=dst, send_sem=send_sem, recv_sem=recv_sem, device_id={"stage": dev}, device_id_type=MESH)


def pipe_kernel(n_stage, half, tile, x0_hbm, emb_hbm, up_hbm, down_hbm, lab_ref,
                n_out, xs_out, hid_out, da_out, g_out, dx0_out, stat_out,
                xbuf, ybuf, abuf, hbuf, nbuf, gbuf, dxbuf, dx0buf, dnbuf, up, down, up_t, down_t,
                emb, zbuf, n_t, dn_acc, dn_send, dn_recv, dn_own, st_send, st_recv, statall,
                w_sem, e_sem, x_sem, f_send, f_recv, n_send, n_recv, ag_send, ag_recv, fw_send,
                st_sems, dp_sems, dn_ssem, dn_rsem, sa_send, sa_recv, b_send, b_recv, d_send, d_recv, r_send, out_sem):
    n_micro, seq, dim = x0_hbm.shape
    ffn = up.shape[1]
    vocab = emb_hbm.shape[0]
    me = lax.axis_index("stage")
    core = lax.rem(me, 2)
    chip = me // 2
    mate = me + 1 - 2 * core
    last_id = n_stage - 1
    first = me == 0
    last = me == last_id
    fblk = 512
    n_fblk = ffn // fblk
    row0 = core * (vocab - half)
    n_tiles = half // tile

    barrier = pltpu.get_barrier_semaphore()
    for d in range(1, n_stage):
        pl.semaphore_signal(barrier, inc=1, device_id={"stage": lax.rem(me + d, n_stage)}, device_id_type=MESH)
    w_copy = [pltpu.make_async_copy(up_hbm, up, w_sem.at[0]), pltpu.make_async_copy(down_hbm, down, w_sem.at[1])]
    for c in w_copy:
        c.start()

    @pl.when(first)
    def _():
        for m in range(n_micro):
            pltpu.make_async_copy(x0_hbm.at[m], xbuf.at[m], x_sem.at[m]).start()

    e_step = half // e_sem.shape[0]

    def e_copy(i):
        src = emb_hbm.at[pl.ds(pl.multiple_of(row0 + i * e_step, LANES), e_step)]
        return pltpu.make_async_copy(src, emb.at[pl.ds(i * e_step, e_step)], e_sem.at[i])

    for i in range(e_sem.shape[0]):
        e_copy(i).start()
    pl.semaphore_wait(barrier, n_stage - 1)
    for c in w_copy:
        c.wait()

    def transpose_weights():
        for j in range(n_fblk):
            up_t[j * fblk:(j + 1) * fblk, :] = up[:, j * fblk:(j + 1) * fblk].T
            down_t[:, j * fblk:(j + 1) * fblk] = down[j * fblk:(j + 1) * fblk, :].T

    @pl.when(chip >= n_stage // 4)
    def _():
        transpose_weights()

    def n_copies(m):
        tgt = 2 * (m // 2)
        return [remote(nbuf.at[m], nbuf.at[m], n_send.at[m, k], n_recv.at[m], tgt + k) for k in range(2)]

    def fwd(m, carry):
        @pl.when(first)
        def _():
            pltpu.make_async_copy(x0_hbm.at[m], xbuf.at[m], x_sem.at[m]).wait()

        @pl.when(jnp.logical_not(first))
        def _():
            remote(xbuf.at[m], xbuf.at[m], f_send.at[m], f_recv.at[m], me).wait_recv()

        x = xbuf[m]
        for j in range(n_fblk):
            cols = slice(j * fblk, (j + 1) * fblk)
            a = dot(x, up[:, cols]).astype(BF16)
            abuf[m, :, cols] = a
            hbuf[m, :, cols] = gelu_fwd(a.astype(F32)).astype(BF16)
        y = (x.astype(F32) + dot(hbuf[m], down[...])).astype(BF16)
        ybuf[m] = y

        @pl.when(jnp.logical_not(last))
        def _():
            remote(ybuf.at[m], xbuf.at[m], f_send.at[m], f_recv.at[m], me + 1).start()

        @pl.when(last)
        def _():
            yf = y.astype(F32)
            inv = lax.rsqrt(jnp.mean(yf * yf, axis=-1, keepdims=True) + EPS)
            nbuf[m] = (yf * inv).astype(BF16)
            copies = n_copies(m)
            copies[0].start()

            @pl.when(m // 2 != last_id // 2)
            def _():
                copies[1].start()

        pltpu.make_async_copy(hbuf.at[m], hid_out.at[m], out_sem.at[0, m]).start()
        pltpu.make_async_copy(xbuf.at[m], xs_out.at[m], out_sem.at[1, m]).start()
        return carry

    lax.fori_loop(0, n_micro, fwd, 0)

    @pl.when(chip < n_stage // 4)
    def _():
        transpose_weights()

    for k in range(2):
        mk = 2 * chip + k

        @pl.when(jnp.logical_not(last))
        def _():
            remote(nbuf.at[mk], nbuf.at[mk], n_send.at[mk, 0], n_recv.at[mk], me).wait_recv()

        n_t[:, k * seq:(k + 1) * seq] = nbuf[mk].T

    peers = [lax.rem(me + 2 * d, n_stage) for d in range(1, n_stage // 2)]
    ag_copies = [remote(nbuf.at[me], nbuf.at[me], ag_send.at[d], ag_recv.at[me], p) for d, p in enumerate(peers)]
    for c, p in zip(ag_copies, peers):
        pl.when(p != last_id)(c.start)
    for i in range(e_sem.shape[0]):
        e_copy(i).wait()

    pair = 2 * seq
    scale = dim ** -0.5
    lab = jnp.concatenate([lab_ref[pl.ds(2 * chip, 1), :], lab_ref[pl.ds(2 * chip + 1, 1), :]], axis=1)
    dup = core * (2 * half - vocab)
    groups = tile // 8

    def logits_step(i, carry):
        top, tot = carry
        rows = pl.ds(pl.multiple_of(i * tile, LANES), tile)
        z = (dot(emb[rows, :], n_t[...]) * scale).astype(BF16)
        local = i * tile + lax.broadcasted_iota(jnp.int32, (tile, pair), 0)
        zf = jnp.where(local >= dup, z.astype(F32), -jnp.inf)
        zbuf[rows, :] = z
        z3 = zf.reshape(groups, 8, pair)
        new_top = jnp.maximum(top, jnp.max(z3, axis=0))
        safe = jnp.where(new_top == -jnp.inf, 0.0, new_top)
        tot = tot * jnp.exp(top - safe) + jnp.sum(jnp.exp(z3 - safe[None]), axis=0)
        return new_top, tot

    top, tot = lax.fori_loop(0, n_tiles, logits_step, (jnp.full((8, pair), -jnp.inf, F32), jnp.zeros((8, pair), F32)))
    row_top = jnp.max(top, axis=0, keepdims=True)
    row_tot = jnp.sum(tot * jnp.exp(top - row_top), axis=0, keepdims=True)
    st_send[0:8, :] = jnp.broadcast_to(row_top, (8, pair))
    st_send[8:16, :] = jnp.broadcast_to(row_tot, (8, pair))
    st_copy = remote(st_send, st_recv, st_sems.at[0], st_sems.at[1], mate)
    st_copy.start()
    st_copy.wait()
    far_top = st_recv[0:1, :]
    far_tot = st_recv[8:9, :]
    all_top = jnp.maximum(row_top, far_top)
    mine = row_tot * jnp.exp(row_top - all_top)
    other = far_tot * jnp.exp(far_top - all_top)
    lse = all_top + jnp.log(jnp.where(core == 0, mine + other, other + mine))
    shift = lse * LOG2E + math.log2(n_micro * seq)
    inv_count = 1.0 / (n_micro * seq)
    dn_acc[...] = jnp.zeros_like(dn_acc)

    def grad_step(i, picked):
        rows = pl.ds(pl.multiple_of(i * tile, LANES), tile)
        zf = zbuf[rows, :].astype(F32)
        local = i * tile + lax.broadcasted_iota(jnp.int32, (tile, pair), 0)
        prob = jnp.exp2(zf * LOG2E - shift)
        hit = local + row0 == lab
        keep = local >= dup
        dz = jnp.where(keep, jnp.where(hit, prob - inv_count, prob), 0.0).astype(BF16)
        dn_acc[...] += dot_t(dz, emb[rows, :])
        got = jnp.where(hit & keep, zf, 0.0).reshape(groups, 8, pair)
        return picked + jnp.sum(got, axis=0)

    picked = lax.fori_loop(0, n_tiles, grad_step, jnp.zeros((8, pair), F32))
    far = pl.ds(pl.multiple_of((1 - core) * seq, seq), seq)
    near = pl.ds(pl.multiple_of(core * seq, seq), seq)
    dn_send[...] = dn_acc[far, :]
    dp_copy = remote(dn_send, dn_recv, dp_sems.at[0], dp_sems.at[1], mate)
    dp_copy.start()
    row_loss = jnp.where(core == 0, lse, 0.0) - jnp.sum(picked, axis=0, keepdims=True)
    pick = lax.broadcasted_iota(jnp.int32, (8, pair), 0)
    statall[me] = jnp.where(pick == 0, lse, jnp.where(pick == 1, row_loss, 0.0))
    sa_copies = [remote(statall.at[me], statall.at[me], sa_send.at[d - 1], sa_recv.at[me], lax.rem(me + d, n_stage)) for d in range(1, n_stage)]
    for c in sa_copies:
        c.start()
    dp_copy.wait()
    dn = ((dn_acc[near, :] + dn_recv[...]) * scale).astype(BF16)
    dn_copy = remote(dn_own, dnbuf.at[me], dn_ssem, dn_rsem.at[me], last_id)

    @pl.when(last)
    def _():
        dnbuf[last_id] = dn

    @pl.when(jnp.logical_not(last))
    def _():
        dn_own[...] = dn
        dn_copy.start()

    for p in peers:
        got = remote(nbuf.at[p], nbuf.at[p], ag_send.at[0], ag_recv.at[p], me)
        pl.when(jnp.logical_not(last))(got.wait_recv)
        pl.when(mate != last_id)(remote(nbuf.at[p], nbuf.at[p], fw_send.at[p], ag_recv.at[p], mate).start)

    dx0_dst = [1] + list(range(2, n_stage, 2))

    def bwd(m, carry):
        @pl.when(jnp.logical_not(last))
        def _():
            remote(gbuf.at[m], gbuf.at[m], b_send.at[m], b_recv.at[m], me).wait_recv()

        @pl.when(last)
        def _():
            @pl.when(m != last_id)
            def _():
                remote(dnbuf.at[m], dnbuf.at[m], dn_ssem, dn_rsem.at[m], me).wait_recv()

            yf = ybuf[m].astype(F32)
            inv = lax.rsqrt(jnp.mean(yf * yf, axis=-1, keepdims=True) + EPS)
            dnf = dnbuf[m].astype(F32)
            proj = jnp.mean(yf * dnf, axis=-1, keepdims=True)
            gbuf[m] = (dnf * inv - yf * (inv * inv * inv * proj)).astype(BF16)

        g = gbuf[m]
        for j in range(n_fblk):
            cols = slice(j * fblk, (j + 1) * fblk)
            dh = dot(g, down_t[:, cols]).astype(BF16).astype(F32)
            abuf[m, :, cols] = (dh * gelu_slope(abuf[m, :, cols].astype(F32))).astype(BF16)
        dxbuf[m] = (g.astype(F32) + dot(abuf[m], up_t[...])).astype(BF16)

        @pl.when(jnp.logical_not(first))
        def _():
            remote(dxbuf.at[m], gbuf.at[m], b_send.at[m], b_recv.at[m], me - 1).start()

        @pl.when(first)
        def _():
            for k, dev in enumerate(dx0_dst):
                remote(dxbuf.at[m], dx0buf.at[m], d_send.at[m, k], d_recv.at[m], dev).start()

        pltpu.make_async_copy(abuf.at[m], da_out.at[m], out_sem.at[2, m]).start()
        pltpu.make_async_copy(gbuf.at[m], g_out.at[m], out_sem.at[3, m]).start()
        return carry

    lax.fori_loop(0, n_micro, bwd, 0)

    def relay(m, carry):
        @pl.when(jnp.logical_not(first))
        def _():
            remote(dx0buf.at[m], dx0buf.at[m], r_send.at[m], d_recv.at[m], me).wait_recv()

            @pl.when(core == 0)
            def _():
                remote(dx0buf.at[m], dx0buf.at[m], r_send.at[m], d_recv.at[m], mate).start()

            pltpu.make_async_copy(dx0buf.at[m], dx0_out.at[m], out_sem.at[4, m]).start()

        @pl.when(first)
        def _():
            pltpu.make_async_copy(dxbuf.at[m], dx0_out.at[m], out_sem.at[4, m]).start()

        return carry

    lax.fori_loop(0, n_micro, relay, 0)

    for d in range(1, n_stage):
        src = lax.rem(me + d, n_stage)
        remote(statall.at[src], statall.at[src], sa_send.at[0], sa_recv.at[src], me).wait_recv()
    for d in range(1, n_stage // 2):
        src = lax.rem(mate + 2 * d, n_stage)
        pl.when(jnp.logical_not(last))(remote(nbuf.at[src], nbuf.at[src], ag_send.at[0], ag_recv.at[src], me).wait_recv)
    outs = [pltpu.make_async_copy(nbuf, n_out, out_sem.at[5, 0]), pltpu.make_async_copy(statall, stat_out, out_sem.at[5, 1])]
    for c in outs:
        c.start()
    for c in sa_copies:
        c.wait_send()
    for c, p in zip(ag_copies, peers):
        pl.when(p != last_id)(c.wait_send)
        pl.when(mate != last_id)(remote(nbuf.at[p], nbuf.at[p], fw_send.at[p], ag_recv.at[p], mate).wait_send)

    @pl.when(jnp.logical_not(last))
    def _():
        dn_copy.wait_send()

    def drain(m, carry):
        @pl.when(jnp.logical_not(last))
        def _():
            remote(ybuf.at[m], xbuf.at[m], f_send.at[m], f_recv.at[m], me).wait_send()

        @pl.when(last)
        def _():
            copies = n_copies(m)
            copies[0].wait_send()

            @pl.when(m // 2 != last_id // 2)
            def _():
                copies[1].wait_send()

        @pl.when(jnp.logical_not(first))
        def _():
            remote(dxbuf.at[m], gbuf.at[m], b_send.at[m], b_recv.at[m], me).wait_send()

            @pl.when(core == 0)
            def _():
                remote(dx0buf.at[m], dx0buf.at[m], r_send.at[m], d_recv.at[m], me).wait_send()

        @pl.when(first)
        def _():
            for k, dev in enumerate(dx0_dst):
                remote(dxbuf.at[m], dx0buf.at[m], d_send.at[m, k], d_recv.at[m], dev).wait_send()

        pltpu.make_async_copy(hbuf.at[m], hid_out.at[m], out_sem.at[0, m]).wait()
        pltpu.make_async_copy(xbuf.at[m], xs_out.at[m], out_sem.at[1, m]).wait()
        pltpu.make_async_copy(abuf.at[m], da_out.at[m], out_sem.at[2, m]).wait()
        pltpu.make_async_copy(gbuf.at[m], g_out.at[m], out_sem.at[3, m]).wait()
        pltpu.make_async_copy(dx0buf.at[m], dx0_out.at[m], out_sem.at[4, m]).wait()
        return carry

    lax.fori_loop(0, n_micro, drain, 0)
    for c in outs:
        c.wait()


def run_pipe(x0, emb, w_up, w_down, labels, n_stage):
    n_micro, seq, dim = x0.shape
    ffn = w_up.shape[1]
    vocab = emb.shape[0]
    half = (vocab // LANES + 1) // 2 * LANES
    tile = next(t for t in (768, 640, 512, 384, 256, 128) if half % t == 0)
    e_parts = next(k for k in (9, 8, 7, 6, 5, 4, 3, 2, 1) if (half // LANES) % k == 0)
    any_spec = pl.BlockSpec(memory_space=pl.ANY)
    act = (n_micro, seq, dim)
    wide = (n_micro, seq, ffn)
    dma = pltpu.SemaphoreType.DMA
    vm = pltpu.VMEM
    pair = 2 * seq
    return pl.pallas_call(
        functools.partial(pipe_kernel, n_stage, half, tile),
        out_shape=[
            jax.ShapeDtypeStruct(act, BF16), jax.ShapeDtypeStruct(act, BF16), jax.ShapeDtypeStruct(wide, BF16),
            jax.ShapeDtypeStruct(wide, BF16), jax.ShapeDtypeStruct(act, BF16), jax.ShapeDtypeStruct(act, BF16),
            jax.ShapeDtypeStruct((n_stage, 8, pair), F32),
        ],
        in_specs=[any_spec] * 4 + [pl.BlockSpec(memory_space=pltpu.VMEM)],
        out_specs=[any_spec] * 7,
        scratch_shapes=[
            vm(act, BF16), vm(act, BF16), vm(wide, BF16), vm(wide, BF16), vm(act, BF16), vm(act, BF16), vm(act, BF16), vm(act, BF16), vm(act, BF16),
            vm((dim, ffn), BF16), vm((ffn, dim), BF16), vm((ffn, dim), BF16), vm((dim, ffn), BF16),
            vm((half, dim), BF16), vm((half, pair), BF16), vm((dim, pair), BF16), vm((pair, dim), F32),
            vm((seq, dim), F32), vm((seq, dim), F32), vm((seq, dim), BF16), vm((16, pair), F32), vm((16, pair), F32), vm((n_stage, 8, pair), F32),
            dma((2,)), dma((e_parts,)), dma((n_micro,)), dma((n_micro,)), dma((n_micro,)), dma((n_micro, 2)), dma((n_micro,)),
            dma((n_stage,)), dma((n_stage,)), dma((n_stage,)),
            dma((2,)), dma((2,)), dma, dma((n_stage,)), dma((n_stage,)), dma((n_stage,)),
            dma((n_micro,)), dma((n_micro,)), dma((n_micro, n_stage // 2)), dma((n_micro,)), dma((n_micro,)), dma((6, n_micro)),
        ],
        compiler_params=pltpu.CompilerParams(collective_id=0, has_side_effects=True, vmem_limit_bytes=66 * 1000 * 1000),
        cost_estimate=pl.CostEstimate(flops=30 * 10**9, bytes_accessed=60 * 10**6, transcendentals=0),
        name="pipe",
    )(x0, emb, w_up, w_down, labels)


def emb_kernel(n_stage, n_tok, bound_ref, e_ref, n_ref, stat_ref, lab_ref, rank_ref, sid_ref, dx0_ref, out_ref, loss_ref, n_t, dx0s, dz, shift):
    i = pl.program_id(0)
    rows, dim = e_ref.shape
    blk = 256
    scale = dim ** -0.5
    inv_count = 1.0 / n_tok

    @pl.when(i == 0)
    def _():
        n_t[...] = n_ref[...].T
        order = lax.broadcasted_iota(jnp.int32, (n_tok, n_tok), 0) == rank_ref[...]
        dx0s[...] = dot(jnp.where(order, 1.0, 0.0).astype(BF16), dx0_ref[...]).astype(BF16)
        pair = stat_ref.shape[2]
        loss = jnp.zeros((1, pair), F32)
        for d in range(n_stage):
            if d % 2 == 0:
                shift[:, (d // 2) * pair:(d // 2 + 1) * pair] = stat_ref[d, 0:1, :] * LOG2E + math.log2(n_tok)
            loss = loss + stat_ref[d, 1:2, :]
        loss_ref[...] = jnp.broadcast_to(jnp.sum(loss, axis=1, keepdims=True) * inv_count, loss_ref.shape)

    e = e_ref[...]
    vid = i * rows + lax.broadcasted_iota(jnp.int32, (rows, blk), 0)
    for j in range(n_tok // blk):
        cols = slice(j * blk, (j + 1) * blk)
        z = (dot(e, n_t[:, cols]) * scale).astype(BF16).astype(F32)
        prob = jnp.exp2(z * LOG2E - shift[:, cols])
        dz[:, cols] = jnp.where(vid == lab_ref[:, cols], prob - inv_count, prob).astype(BF16)
    out_ref[...] = dot(dz[...], n_ref[...]) * scale

    lo = bound_ref[i]
    hi = bound_ref[i + 1]

    def add_rows(c, carry):
        ids = sid_ref[pl.ds(c, 1), :]
        hot = jnp.where(i * rows + lax.broadcasted_iota(jnp.int32, (rows, LANES), 0) == ids, 1.0, 0.0).astype(BF16)
        out_ref[...] += dot(hot, dx0s[pl.ds(pl.multiple_of(c * LANES, LANES), LANES), :])
        return carry

    lax.fori_loop(lo // LANES, jnp.where(hi > lo, (hi + LANES - 1) // LANES, lo // LANES), add_rows, 0)


def run_emb(emb, n_all, stats, labels, tokens, dx0, n_stage):
    vocab, dim = emb.shape
    n_tok = n_all.shape[0]
    rows = 1024
    steps = pl.cdiv(vocab, rows)
    pos = jnp.arange(n_tok, dtype=jnp.int32)
    tc, tr = tokens[:, None], tokens[None, :]
    before = (tr < tc) | ((tr == tc) & (pos[None, :] < pos[:, None]))
    rank = jnp.sum(before.astype(jnp.int32), axis=1)
    sid = jnp.sum(jnp.where(rank[None, :] == pos[:, None], tr, 0), axis=1)
    bounds = jnp.sum((tr < (jnp.arange(steps + 1, dtype=jnp.int32) * rows)[:, None]).astype(jnp.int32), axis=1)
    full = lambda *shape: pl.BlockSpec(shape, lambda i, b: (0,) * len(shape))
    return pl.pallas_call(
        functools.partial(emb_kernel, n_stage, n_tok),
        out_shape=[jax.ShapeDtypeStruct((vocab, dim), F32), jax.ShapeDtypeStruct((8, LANES), F32)],
        grid_spec=pltpu.PrefetchScalarGridSpec(
            num_scalar_prefetch=1,
            grid=(steps,),
            in_specs=[
                pl.BlockSpec((rows, dim), lambda i, b: (i, 0)),
                full(n_tok, dim), full(*stats.shape), full(1, n_tok), full(1, n_tok), full(n_tok // LANES, LANES), full(n_tok, dim),
            ],
            out_specs=[pl.BlockSpec((rows, dim), lambda i, b: (i, 0)), full(8, LANES)],
            scratch_shapes=[pltpu.VMEM((dim, n_tok), BF16), pltpu.VMEM((n_tok, dim), BF16), pltpu.VMEM((rows, n_tok), BF16), pltpu.VMEM((1, n_tok), F32)],
        ),
        compiler_params=pltpu.CompilerParams(vmem_limit_bytes=60 * 1000 * 1000),
        cost_estimate=pl.CostEstimate(flops=4 * n_tok * vocab * dim, bytes_accessed=6 * vocab * dim, transcendentals=0),
        name="emb",
    )(bounds, emb, n_all, stats, labels[None, :], rank[None, :], sid.reshape(n_tok // LANES, LANES), dx0)


def solution(mesh):
    n_stage = mesh.shape["stage"]

    def device_fn(tokens, labels, emb, w_up, w_down):
        n_micro, seq = tokens.shape
        dim = emb.shape[1]
        w_up, w_down = w_up[0], w_down[0]
        ffn = w_up.shape[1]
        n_tok = n_micro * seq
        flat = tokens.reshape(n_tok)
        x0 = jnp.take(emb, flat, axis=0).reshape(n_micro, seq, dim)
        n_all, xs, hid, da, g, dx0, stats = run_pipe(x0, emb, w_up, w_down, labels, n_stage)
        grad_emb, loss = run_emb(emb, n_all.reshape(n_tok, dim), stats, labels.reshape(n_tok), flat, dx0.reshape(n_tok, dim), n_stage)
        over = lambda p, q: lax.dot_general(p.reshape(n_tok, -1), q.reshape(n_tok, -1), (((0,), (0,)), ((), ())), preferred_element_type=F32)
        return loss[0, :1], over(xs, da)[None], over(hid, g)[None], grad_emb

    return jax.shard_map(device_fn, mesh=mesh, in_specs=(P("dp", None), P("dp", None), P(None, None), P("stage", None, None), P("stage", None, None)), out_specs=(P("dp"), P(("dp", "stage"), None, None), P(("dp", "stage"), None, None), P("dp", None)), check_vma=False)
```

time: 2250 us -> 259 us (0.12); the launches traced: 2220 us -> 259 us
  starting transfers between devices: 919 us -> 0 us
  waiting for transfers between devices: 656 us -> 0 us
  other arithmetic: 383 us -> 7.35 us
  Pallas kernels: 0 us -> 225 us
  local copies, waits for them, and re-layouts: 119 us -> 14.2 us
  matrix products: 98.3 us -> 11.5 us
  blocking collectives: 29.8 us -> 0 us
    ppermute x44 -> x0, starting transfers between devices: 919 us -> none  [the longest x22 809 us: tick(): recv_act = lax.ppermute(y_out, 'stage', fwd_perm)]
    psum x1 -> x0, waiting for transfers between devices: 623 us -> none  [device_fn(): grad_emb = lax.psum(final_state[7], 'stage')]
    scatter-add x22 -> x0, other arithmetic: 350 us -> none  [tick(): grad_emb = grad_emb.at[tok_b].add(emb_rows)]
    pallas_call x0 -> x2, Pallas kernels: none -> 225 us  [the longest x1 125 us: run_pipe(): pl.pallas_call(functools.partial(pipe_kernel, n_stage, half, tile), out_s...]
    dot_general x48 -> x2, matrix products: 98.3 us -> 11.5 us  [device_fn(): lax.dot_general(p.reshape(n_tok, -1), q.reshape(n_tok, -1), (((0,), (0,))...]
    unnamed x3 -> x6, local copies, waits for them, and re-layouts: 43.1 us -> 0.01 us
    ppermute x44 -> x0, waiting for transfers between devices: 32.7 us -> none  [the longest x22 32.7 us: tick(): recv_grad = lax.ppermute(grad_in, 'stage', bwd_perm)]
    psum x1 -> x0, blocking collectives: 29.8 us -> none  [device_fn(): loss_total = lax.psum(final_state[8], 'stage')]
  transfers between devices with their start and end apart: 45 -> 0, of which waited for: 9 -> 0; matrix products, arithmetic and copies ran while one was open for 19% -> 0% of each run, Pallas kernels for 0% -> 0%
where the time goes in v1:
time: 259 us
  Pallas kernels  225 us (87%)
  local copies, waits for them, and re-layouts  14.2 us (5%)
  matrix products  11.5 us (4%)
  other arithmetic  7.35 us (3%)
    pallas_call x1, Pallas kernels, run_pipe(): pl.pallas_call(functools.partial(pipe_kernel, n_stage, half, tile), out_s...  125 us
    pallas_call x1, Pallas kernels, run_emb(): pl.pallas_call(functools.partial(emb_kernel, n_stage, n_tok), out_shape=[...  100 us
    gather x1, local copies, waits for them, and re-layouts, device_fn(): x0 = jnp.take(emb, flat, axis=0).reshape(n_micro, seq, dim)  13 us
    dot_general x2, matrix products, device_fn(): lax.dot_general(p.reshape(n_tok, -1), q.reshape(n_tok, -1), (((0,), (0,))...  11.5 us

profile of v1, /device:TPU:125, one launch (start us, length us, event | category | flops | bytes accessed | tf_op | source)
XLA Modules:
  0.0 258.6 jit_solution(11672986423279891137)
XLA Ops:
  0.6 1.4 convert_reduce_fusion.1.bound_ref
  2.0 0.7 compare_and_fusion
  2.7 1.6 convert_reduce_fusion
  4.3 0.0 copy-start
  4.3 1.8 select_reduce_fusion
  6.1 0.7 compare_select_fusion
  6.8 13.0 %gather_fusion = bf16[1024,512]{1,0:T(8,128)(2,1)S(1)} fusion(bf16[32128,512]{1,0:T(8,128)(2,1)} %e_ref.1, s32[1024]{0:T(1024)S(1)} %broadcast_clamp_fusion), kind=kCustom, calls=%fused_computation | custom fusion | bytes 2101248 | tf_op jit(solution)/shard_map/jit(_take)/gather | solution.py:479
  19.8 0.0 copy-done
  19.8 1.2 broadcast_select_fusion.x0_hbm
  21.0 124.6 %pipe.1 = (bf16[8,128,512]{2,1,0:T(8,128)(2,1)}, bf16[8,128,512]{2,1,0:T(8,128)(2,1)}, bf16[8,128,2048]{2,1,0:T(8,128)(2,1)}, bf16[8,128,2048]{2,1,0:T(8,128)(2,...) custom-call(bf16[8,128,512]{2,1,0:T(8,128)(2,1)} %broadcast_select_fusion.x0_hbm, ...), custom_call_target="tpu_custom_call" | custom-call | flops 30000001024 | bytes 60000000 | tf_op jit(solution)/shard_map/pipe/pallas_call | solution.py:372
  145.6 0.0 copy-start.1
  145.6 0.0 copy-start.2
  145.7 7.0 %convolution_bitcast_fusion.1 = f32[1,512,2048]{2,1,0:T(8,128)} fusion(bf16[8,128,512]{2,1,0:T(8,128)(2,1)} %get-tuple-element.17, bf16[8,128,2048]{2,1,0:T(8,128)(2,1)} %get-tuple-element.18), kind=kOutput, calls=%fused_computation.8 | convolution fusion | flops 2147483648 | bytes 9437184 | tf_op jit(solution)/shard_map/dot_general | solution.py:482
  152.7 0.0 copy-done.1
  152.7 0.0 copy-done.2
  152.7 4.4 %convolution_bitcast_fusion = f32[1,2048,512]{2,1,0:T(8,128)} fusion(bf16[8,128,2048]{2,1,0:T(8,128)(2,1)S(1)} %copy-done.1, bf16[8,128,512]{2,1,0:T(8,128)(2,1)S(1)} %copy-done.2), kind=kOutput, calls=%fused_computation.7 | convolution fusion | flops 2147483648 | bytes 9437184 | tf_op jit(solution)/shard_map/dot_general | solution.py:482
  157.2 100.3 %emb.1 = (f32[32128,512]{1,0:T(8,128)}, f32[8,128]{1,0:T(8,128)}) custom-call(s32[33]{0:T(128)} %convert_reduce_fusion.1.bound_ref, bf16[32128,512]{1,0:T(8,128)(2,1)} %e_ref.1, bf16[1024,512]{1,0:T(8,128)(2,1)} %bitcast.33, f32[8,8,256]{2,1,0:T(8,128)} %get-tuple-element.14.stat_ref, s32[1,1024]{1,0:T(1,128)} %bitcast.32, s32[1,1024]{1,0:T(1,128)} %bitcast.28, ...), custom_call_target="tpu_custom_call" | custom-call | flops 67377299456 | bytes 98697216 | tf_op jit(solution)/shard_map/emb/pallas_call | solution.py:450
  257.4 1.2 slice.3
  (2 shorter events, 0.0 us)
Async XLA Ops:
  4.3 15.5 %copy-start = (s32[1024]{0:T(1024)}, s32[1024]{0:T(1024)S(1)}, u32[]{:S(2)}) copy-start(s32[1024]{0:T(1024)S(1)} %convert_reduce_fusion) | copy-start | bytes 12292
  145.6 7.1 %copy-start.1 = (bf16[8,128,2048]{2,1,0:T(8,128)(2,1)S(1)}, bf16[8,128,2048]{2,1,0:T(8,128)(2,1)}, u32[]{:S(2)}) copy-start(bf16[8,128,2048]{2,1,0:T(8,128)(2,1)} %get-tuple-element.19) | copy-start | bytes 12582916
  145.6 7.1 %copy-start.2 = (bf16[8,128,512]{2,1,0:T(8,128)(2,1)S(1)}, bf16[8,128,512]{2,1,0:T(8,128)(2,1)}, u32[]{:S(2)}) copy-start(bf16[8,128,512]{2,1,0:T(8,128)(2,1)} %get-tuple-element.20) | copy-start | bytes 3145732

commit v2 on v1

v2 whole, which is shorter than its diff:
```python
import functools
import math

import jax
import jax.numpy as jnp
from jax import lax
from jax.experimental import pallas as pl
from jax.experimental.pallas import tpu as pltpu
from jax.sharding import PartitionSpec as P

MESH = pl.DeviceIdType.MESH
LOG2E = math.log2(math.e)
LN2 = math.log(2.0)
GELU_C = math.sqrt(2.0 / math.pi)
GELU_K = 0.044715
EPS = 1e-6
LANES = 128
F32 = jnp.float32
BF16 = jnp.bfloat16


def gelu_fwd(a):
    return 0.5 * a * (1.0 + jnp.tanh(GELU_C * (a + GELU_K * (a * a * a))))


def gelu_slope(a):
    a2 = a * a
    t = jnp.tanh(GELU_C * (a + GELU_K * (a2 * a)))
    return 0.5 * (1.0 + t) + (0.5 * a) * (1.0 - t * t) * (GELU_C + (3.0 * GELU_C * GELU_K) * a2)


def dot(x, y):
    return jnp.dot(x, y, preferred_element_type=F32)


def dot_t(x, y):
    return lax.dot_general(x, y, (((0,), (0,)), ((), ())), preferred_element_type=F32)


def remote(src, dst, send_sem, recv_sem, dev):
    return pltpu.make_async_remote_copy(src_ref=src, dst_ref=dst, send_sem=send_sem, recv_sem=recv_sem, device_id={"stage": dev}, device_id_type=MESH)


def gather_kernel(n_stage, ids_ref, row_ref, tok_ref, cut_ref, emb_hbm, x0_out, rank_out, sid_out, cnt_out, tiles, sem):
    n_micro, seq = tok_ref.shape
    n_tok = n_micro * seq
    me = lax.axis_index("stage")
    group = tiles.shape[1] // seq
    slots = tiles.shape[0]
    owners = [head_chunk(me, k, n_micro) for k in range(slots)]

    def fetch(k):
        def one(i, carry):
            t = ids_ref[owners[k] * seq + i]
            start = pl.multiple_of(t // group * group, group)
            pltpu.make_async_copy(emb_hbm.at[pl.ds(start, group)], tiles.at[k, pl.ds(pl.multiple_of(i * group, group), group)], sem.at[k]).start()
            return carry

        lax.fori_loop(0, seq, one, 0, unroll=8)

    fetch(0)
    for k in range(1, slots):
        pl.when(me < slots)(functools.partial(fetch, k))

    def column(row):
        return jnp.broadcast_to(row, (LANES, LANES)).T

    sub = lax.broadcasted_iota(jnp.int32, (LANES, LANES), 0)
    lane = lax.broadcasted_iota(jnp.int32, (LANES, LANES), 1)
    tok_row = row_ref[...]
    key_row = tok_row * n_tok + lax.broadcasted_iota(jnp.int32, (1, n_tok), 1)
    n_grp = n_tok // LANES
    cols = [column(tok_row[:, c * LANES:(c + 1) * LANES].astype(F32)) for c in range(n_grp)]
    keys = [cols[c].astype(jnp.int32) * n_tok + (sub + c * LANES) for c in range(n_grp)]
    ranks = []
    for g in range(n_grp):
        mine = key_row[:, g * LANES:(g + 1) * LANES]
        acc = jnp.zeros((LANES, LANES), F32)
        for c in range(n_grp):
            acc = acc + jnp.where(keys[c] < mine, 1.0, 0.0)
        ranks.append(jnp.sum(acc, axis=0, keepdims=True))
        rank_out[:, g * LANES:(g + 1) * LANES] = ranks[g].astype(jnp.int32)
    rank_cols = [column(r) for r in ranks]
    for g in range(n_grp):
        want = (lane + g * LANES).astype(F32)
        acc = jnp.zeros((LANES, LANES), F32)
        for c in range(n_grp):
            acc = acc + jnp.where(rank_cols[c] == want, cols[c], 0.0)
        sid_out[g:g + 1, :] = jnp.sum(acc, axis=0, keepdims=True).astype(jnp.int32)
    cut = cut_ref[...].astype(F32)
    acc = jnp.zeros((LANES, LANES), F32)
    for c in range(n_grp):
        acc = acc + jnp.where(cols[c] < cut, 1.0, 0.0)
    cnt_out[...] = jnp.sum(acc, axis=0, keepdims=True).astype(jnp.int32)

    def select(k):
        pltpu.make_async_copy(emb_hbm.at[pl.ds(0, seq * group)], tiles.at[k], sem.at[k]).wait()
        tok = column(tok_ref[pl.ds(owners[k], 1), :].astype(F32)).astype(jnp.int32)
        want = sub * group + (tok - tok // group * group)
        hot = [jnp.where(lane + b * LANES == want, 1.0, 0.0).astype(BF16) for b in range(seq * group // LANES)]
        x0_out[k] = dot(jnp.concatenate(hot, axis=1), tiles[k]).astype(BF16)

    select(0)
    for k in range(1, slots):
        pl.when(me < slots)(functools.partial(select, k))


def head_chunk(dev, k, n_micro):
    return jnp.minimum(jnp.where(dev < 2, 2 * dev + k, dev + 2), n_micro - 1)


def run_gather(tokens, emb, cuts, n_stage):
    n_micro, seq = tokens.shape
    n_tok = n_micro * seq
    dim = emb.shape[1]
    group = 16
    vspec = pl.BlockSpec(memory_space=pltpu.VMEM)
    return pl.pallas_call(
        functools.partial(gather_kernel, n_stage),
        out_shape=[
            jax.ShapeDtypeStruct((2, seq, dim), BF16), jax.ShapeDtypeStruct((1, n_tok), jnp.int32),
            jax.ShapeDtypeStruct((n_tok // LANES, LANES), jnp.int32), jax.ShapeDtypeStruct((1, LANES), jnp.int32),
        ],
        in_specs=[pl.BlockSpec(memory_space=pltpu.SMEM), vspec, vspec, vspec, pl.BlockSpec(memory_space=pl.ANY)],
        out_specs=[vspec] * 4,
        scratch_shapes=[pltpu.VMEM((2, seq * group, dim), BF16), pltpu.SemaphoreType.DMA((2,))],
        compiler_params=pltpu.CompilerParams(vmem_limit_bytes=32 * 1000 * 1000),
        cost_estimate=pl.CostEstimate(flops=10**9, bytes_accessed=2 * seq * group * dim * 2, transcendentals=0),
        name="gather",
    )(tokens.reshape(n_tok), tokens.reshape(1, n_tok), tokens, cuts, emb)


def logit_grad(e, n_t, shift, lab, first_id, inv_count, scale, dz):
    rows = e.shape[0]
    n_tok = n_t.shape[1]
    blk = 256
    vid = lax.broadcasted_iota(jnp.int32, (rows, blk), 0)
    for j in range(n_tok // blk):
        cols = slice(j * blk, (j + 1) * blk)
        z = (dot(e, n_t[:, cols]) * scale).astype(BF16).astype(F32)
        prob = jnp.exp2(z * LOG2E - shift[:, cols])
        dz[:, cols] = jnp.where(vid == lab[:, cols] - first_id, prob - inv_count, prob).astype(BF16)


def pipe_kernel(n_stage, plan, x0_hbm, emb_hbm, up_hbm, down_hbm, lab_ref,
                n_out, xs_out, hid_out, da_out, g_out, dx0_out, stat_out, tmp_out,
                xbuf, ybuf, abuf, hbuf, nbuf, gbuf, dxbuf, dx0buf, dnbuf, up, down, up_t, down_t,
                emb, zbuf, n_t, dn_acc, dn_send, dn_recv, dn_own, st_send, st_recv, statall, tops, n_all_t, shift, dz, obuf,
                w_sem, e_sem, x_sem, f_send, f_recv, n_send, n_recv, ag_send, ag_recv, fw_send,
                st_sems, dp_sems, dn_ssem, dn_rsem, sa_send, sa_recv, b_send, b_recv, d_send, d_recv, r_send, out_sem, x_send, o_sem, od_send, od_recv):
    n_micro, seq, dim = xbuf.shape
    n_tok = n_micro * seq
    ffn = up.shape[1]
    vocab = emb_hbm.shape[0]
    me = lax.axis_index("stage")
    core = lax.rem(me, 2)
    chip = me // 2
    mate = me + 1 - 2 * core
    last_id = n_stage - 1
    first = me == 0
    last = me == last_id
    fblk = 512
    n_fblk = ffn // fblk
    base, extra, tile = plan.base, plan.extra, plan.head_tile
    row0 = core * (base + extra)
    n_tiles = base // tile

    barrier = pltpu.get_barrier_semaphore()
    for d in range(1, n_stage):
        pl.semaphore_signal(barrier, inc=1, device_id={"stage": lax.rem(me + d, n_stage)}, device_id_type=MESH)
    w_copy = [pltpu.make_async_copy(up_hbm, up, w_sem.at[0]), pltpu.make_async_copy(down_hbm, down, w_sem.at[1])]
    for c in w_copy:
        c.start()
    x_slots = x0_hbm.shape[0]
    x_mine = [head_chunk(me, k, n_micro) for k in range(x_slots)]

    @pl.when(first)
    def _():
        for k in range(x_slots):
            pltpu.make_async_copy(x0_hbm.at[k], xbuf.at[k], x_sem.at[k]).start()

    e_parts = e_sem.shape[0] - 1
    e_step = base // e_parts

    def e_copy(i):
        src = emb_hbm.at[pl.ds(pl.multiple_of(row0 + i * e_step, 16), e_step)]
        return pltpu.make_async_copy(src, emb.at[pl.ds(i * e_step, e_step)], e_sem.at[i])

    e_more = pltpu.make_async_copy(emb_hbm.at[pl.ds(base, extra)], emb.at[pl.ds(base, extra)], e_sem.at[e_parts])
    for i in range(e_parts):
        e_copy(i).start()
    pl.when(core == 0)(e_more.start)
    pl.semaphore_wait(barrier, n_stage - 1)

    def x_copy(k):
        return remote(x0_hbm.at[k], xbuf.at[x_mine[k]], x_send.at[k], f_recv.at[x_mine[k]], 0)

    @pl.when(jnp.logical_not(first) & (me + 2 < n_micro))
    def _():
        x_copy(0).start()

        @pl.when(me < 2)
        def _():
            x_copy(1).start()

    for c in w_copy:
        c.wait()

    def transpose_weights():
        for j in range(n_fblk):
            up_t[j * fblk:(j + 1) * fblk, :] = up[:, j * fblk:(j + 1) * fblk].T
            down_t[:, j * fblk:(j + 1) * fblk] = down[j * fblk:(j + 1) * fblk, :].T

    @pl.when(chip >= n_stage // 4)
    def _():
        transpose_weights()

    def n_copies(m):
        tgt = 2 * (m // 2)
        return [remote(nbuf.at[m], nbuf.at[m], n_send.at[m, k], n_recv.at[m], tgt + k) for k in range(2)]

    def fwd(m, carry):
        local = first & (m < x_slots)

        @pl.when(local)
        def _():
            pltpu.make_async_copy(x0_hbm.at[m], xbuf.at[m], x_sem.at[m]).wait()

        @pl.when(jnp.logical_not(local))
        def _():
            remote(xbuf.at[m], xbuf.at[m], f_send.at[m], f_recv.at[m], me).wait_recv()

        x = xbuf[m]
        for j in range(n_fblk):
            cols = slice(j * fblk, (j + 1) * fblk)
            a = dot(x, up[:, cols]).astype(BF16)
            abuf[m, :, cols] = a
            hbuf[m, :, cols] = gelu_fwd(a.astype(F32)).astype(BF16)
        y = (x.astype(F32) + dot(hbuf[m], down[...])).astype(BF16)
        ybuf[m] = y

        @pl.when(jnp.logical_not(last))
        def _():
            remote(ybuf.at[m], xbuf.at[m], f_send.at[m], f_recv.at[m], me + 1).start()

        @pl.when(last)
        def _():
            yf = y.astype(F32)
            inv = lax.rsqrt(jnp.mean(yf * yf, axis=-1, keepdims=True) + EPS)
            nbuf[m] = (yf * inv).astype(BF16)
            copies = n_copies(m)
            copies[0].start()

            @pl.when(m // 2 != last_id // 2)
            def _():
                copies[1].start()

        pltpu.make_async_copy(hbuf.at[m], hid_out.at[m], out_sem.at[0, m]).start()
        pltpu.make_async_copy(xbuf.at[m], xs_out.at[m], out_sem.at[1, m]).start()
        return carry

    lax.fori_loop(0, n_micro, fwd, 0)

    @pl.when(chip < n_stage // 4)
    def _():
        transpose_weights()

    for k in range(2):
        mk = 2 * chip + k

        @pl.when(jnp.logical_not(last))
        def _():
            remote(nbuf.at[mk], nbuf.at[mk], n_send.at[mk, 0], n_recv.at[mk], me).wait_recv()

        n_t[:, k * seq:(k + 1) * seq] = nbuf[mk].T

    peers = [lax.rem(me + 2 * d, n_stage) for d in range(1, n_stage // 2)]
    ag_copies = [remote(nbuf.at[me], nbuf.at[me], ag_send.at[d], ag_recv.at[me], p) for d, p in enumerate(peers)]
    for c, p in zip(ag_copies, peers):
        pl.when(p != last_id)(c.start)
    for i in range(e_parts):
        e_copy(i).wait()
    pl.when(core == 0)(e_more.wait)

    pair = 2 * seq
    scale = dim ** -0.5
    inv_count = 1.0 / n_tok
    log_count = math.log2(n_tok)
    lab = lab_ref[:, pl.ds(pl.multiple_of(chip * pair, pair), pair)]

    def logits(rows, size, top, tot):
        z = (dot(emb[rows, :], n_t[...]) * scale).astype(BF16)
        zbuf[rows, :] = z
        z3 = z.astype(F32).reshape(size // 8, 8, pair)
        new_top = jnp.maximum(top, jnp.max(z3, axis=0))
        off = new_top * LOG2E
        return new_top, tot * jnp.exp2(top * LOG2E - off) + jnp.sum(jnp.exp2(z3 * LOG2E - off[None]), axis=0)

    tops[0] = jnp.full((8, pair), -jnp.inf, F32)
    tops[1] = jnp.zeros((8, pair), F32)

    @pl.when(core == 0)
    def _():
        tops[0], tops[1] = logits(pl.ds(base, extra), extra, tops[0], tops[1])

    top, tot = lax.fori_loop(0, n_tiles, lambda i, c: logits(pl.ds(pl.multiple_of(i * tile, 16), tile), tile, *c), (tops[0], tops[1]))
    row_top = jnp.max(top, axis=0, keepdims=True)
    row_tot = jnp.sum(tot * jnp.exp2((top - row_top) * LOG2E), axis=0, keepdims=True)
    st_send[0:8, :] = jnp.broadcast_to(row_top, (8, pair))
    st_send[8:16, :] = jnp.broadcast_to(row_tot, (8, pair))
    st_copy = remote(st_send, st_recv, st_sems.at[0], st_sems.at[1], mate)
    st_copy.start()
    st_copy.wait()
    far_top = st_recv[0:1, :]
    far_tot = st_recv[8:9, :]
    all_top = jnp.maximum(row_top, far_top)
    mine = row_tot * jnp.exp(row_top - all_top)
    other = far_tot * jnp.exp(far_top - all_top)
    lse = all_top + jnp.log(jnp.where(core == 0, mine + other, other + mine))
    my_shift = lse * LOG2E + log_count

    def grads(rows, size, first_row, picked):
        zf = zbuf[rows, :].astype(F32)
        prob = jnp.exp2(zf * LOG2E - my_shift)
        hit = lax.broadcasted_iota(jnp.int32, (size, pair), 0) == lab - (row0 + first_row)
        dz_t = jnp.where(hit, prob - inv_count, prob).astype(BF16)
        got = jnp.where(hit, zf, 0.0).reshape(size // 8, 8, pair)
        return dot_t(dz_t, emb[rows, :]), picked + jnp.sum(got, axis=0)

    tops[0] = jnp.zeros((8, pair), F32)
    dn_acc[...] = jnp.zeros_like(dn_acc)

    @pl.when(core == 0)
    def _():
        dn_acc[...], tops[0] = grads(pl.ds(base, extra), extra, base, tops[0])

    def grad_step(i, picked):
        part, picked = grads(pl.ds(pl.multiple_of(i * tile, 16), tile), tile, i * tile, picked)
        dn_acc[...] += part
        return picked

    picked = lax.fori_loop(0, n_tiles, grad_step, tops[0])
    far = pl.ds(pl.multiple_of((1 - core) * seq, seq), seq)
    near = pl.ds(pl.multiple_of(core * seq, seq), seq)
    dn_send[...] = dn_acc[far, :]
    dp_copy = remote(dn_send, dn_recv, dp_sems.at[0], dp_sems.at[1], mate)
    dp_copy.start()
    row_loss = jnp.where(core == 0, lse, 0.0) - jnp.sum(picked, axis=0, keepdims=True)
    pick = lax.broadcasted_iota(jnp.int32, (8, pair), 0)
    statall[me] = jnp.where(pick == 0, lse, jnp.where(pick == 1, row_loss, 0.0))
    sa_copies = [remote(statall.at[me], statall.at[me], sa_send.at[d - 1], sa_recv.at[me], lax.rem(me + d, n_stage)) for d in range(1, n_stage)]
    for c in sa_copies:
        c.start()
    dp_copy.wait()
    dn = ((dn_acc[near, :] + dn_recv[...]) * scale).astype(BF16)
    dn_copy = remote(dn_own, dnbuf.at[me], dn_ssem, dn_rsem.at[me], last_id)

    @pl.when(last)
    def _():
        dnbuf[last_id] = dn

    @pl.when(jnp.logical_not(last))
    def _():
        dn_own[...] = dn
        dn_copy.start()

    for p in peers:
        got = remote(nbuf.at[p], nbuf.at[p], ag_send.at[0], ag_recv.at[p], me)
        pl.when(jnp.logical_not(last))(got.wait_recv)
        pl.when(mate != last_id)(remote(nbuf.at[p], nbuf.at[p], fw_send.at[p], ag_recv.at[p], mate).start)

    dx0_dst = [1] + list(range(2, n_stage, 2))

    def bwd(m):
        @pl.when(jnp.logical_not(last))
        def _():
            remote(gbuf.at[m], gbuf.at[m], b_send.at[m], b_recv.at[m], me).wait_recv()

        @pl.when(last)
        def _():
            @pl.when(m != last_id)
            def _():
                remote(dnbuf.at[m], dnbuf.at[m], dn_ssem, dn_rsem.at[m], me).wait_recv()

            yf = ybuf[m].astype(F32)
            inv = lax.rsqrt(jnp.mean(yf * yf, axis=-1, keepdims=True) + EPS)
            dnf = dnbuf[m].astype(F32)
            proj = jnp.mean(yf * dnf, axis=-1, keepdims=True)
            gbuf[m] = (dnf * inv - yf * (inv * inv * inv * proj)).astype(BF16)

        g = gbuf[m]
        for j in range(n_fblk):
            cols = slice(j * fblk, (j + 1) * fblk)
            dh = dot(g, down_t[:, cols]).astype(BF16).astype(F32)
            abuf[m, :, cols] = (dh * gelu_slope(abuf[m, :, cols].astype(F32))).astype(BF16)
        dxbuf[m] = (g.astype(F32) + dot(abuf[m], up_t[...])).astype(BF16)

        @pl.when(jnp.logical_not(first))
        def _():
            remote(dxbuf.at[m], gbuf.at[m], b_send.at[m], b_recv.at[m], me - 1).start()

        @pl.when(first)
        def _():
            for k, dev in enumerate(dx0_dst):
                remote(dxbuf.at[m], dx0buf.at[m], d_send.at[m, k], d_recv.at[m], dev).start()

        pltpu.make_async_copy(abuf.at[m], da_out.at[m], out_sem.at[2, m]).start()
        pltpu.make_async_copy(gbuf.at[m], g_out.at[m], out_sem.at[3, m]).start()

    def tile_copies(k, slot):
        rows = pl.ds(pl.multiple_of(k * plan.rows, plan.rows), plan.rows)
        own = pltpu.make_async_copy(obuf.at[slot], tmp_out.at[core, rows], o_sem.at[slot])
        return own, remote(obuf.at[slot], tmp_out.at[core, rows], od_send.at[k], od_recv.at[k], mate)

    def emb_tile(k):
        @pl.when(k == 0)
        def _():
            for d in range(1, n_stage):
                src = lax.rem(me + d, n_stage)
                remote(statall.at[src], statall.at[src], sa_send.at[0], sa_recv.at[src], me).wait_recv()
            for d in range(1, n_stage // 2):
                src = lax.rem(mate + 2 * d, n_stage)
                pl.when(jnp.logical_not(last))(remote(nbuf.at[src], nbuf.at[src], ag_send.at[0], ag_recv.at[src], me).wait_recv)
            for m in range(n_micro):
                n_all_t[:, m * seq:(m + 1) * seq] = nbuf[m].T
            for c in range(n_stage // 2):
                shift[:, c * pair:(c + 1) * pair] = statall[2 * c, 0:1, :] * LOG2E + log_count

        slot = lax.rem(k, 2)

        @pl.when(k >= 2)
        def _():
            own, far_copy = tile_copies(k - 2, slot)
            own.wait()
            far_copy.wait_send()

        rows = pl.ds(pl.multiple_of(k * plan.rows, plan.rows), plan.rows)
        logit_grad(emb[rows, :], n_all_t, shift, lab_ref, row0 + k * plan.rows, inv_count, scale, dz)
        obuf[slot] = dot(dz[...], nbuf[...].reshape(n_tok, dim)) * scale
        own, far_copy = tile_copies(k, slot)
        own.start()
        far_copy.start()

    before = sum(jnp.where(me == s, plan.before[s], 0) for s in range(n_stage))

    def work(i, carry):
        chunk = (i >= before) & (i < before + n_micro)
        pl.when(chunk)(lambda: bwd(i - before))
        pl.when(jnp.logical_not(chunk))(lambda: emb_tile(jnp.where(i < before, i, i - n_micro)))
        return carry

    lax.fori_loop(0, plan.tiles + n_micro, work, 0)
    outs = [pltpu.make_async_copy(nbuf, n_out, out_sem.at[5, 0]), pltpu.make_async_copy(statall, stat_out, out_sem.at[5, 1])]
    for c in outs:
        c.start()

    def relay(m, carry):
        @pl.when(jnp.logical_not(first))
        def _():
            remote(dx0buf.at[m], dx0buf.at[m], r_send.at[m], d_recv.at[m], me).wait_recv()

            @pl.when(core == 0)
            def _():
                remote(dx0buf.at[m], dx0buf.at[m], r_send.at[m], d_recv.at[m], mate).start()

            pltpu.make_async_copy(dx0buf.at[m], dx0_out.at[m], out_sem.at[4, m]).start()

        @pl.when(first)
        def _():
            pltpu.make_async_copy(dxbuf.at[m], dx0_out.at[m], out_sem.at[4, m]).start()

        return carry

    lax.fori_loop(0, n_micro, relay, 0)

    for k in range(max(plan.tiles - 2, 0), plan.tiles):
        own, far_copy = tile_copies(k, k % 2)
        own.wait()
        far_copy.wait_send()
    for k in range(plan.tiles):
        rows = pl.ds(k * plan.rows, plan.rows)
        remote(obuf.at[0], tmp_out.at[1 - core, rows], od_send.at[k], od_recv.at[k], me).wait_recv()
    for c in sa_copies:
        c.wait_send()
    for c, p in zip(ag_copies, peers):
        pl.when(p != last_id)(c.wait_send)
        pl.when(mate != last_id)(remote(nbuf.at[p], nbuf.at[p], fw_send.at[p], ag_recv.at[p], mate).wait_send)

    @pl.when(jnp.logical_not(last))
    def _():
        dn_copy.wait_send()

    @pl.when(jnp.logical_not(first) & (me + 2 < n_micro))
    def _():
        x_copy(0).wait_send()

        @pl.when(me < 2)
        def _():
            x_copy(1).wait_send()

    def drain(m, carry):
        @pl.when(jnp.logical_not(last))
        def _():
            remote(ybuf.at[m], xbuf.at[m], f_send.at[m], f_recv.at[m], me).wait_send()

        @pl.when(last)
        def _():
            copies = n_copies(m)
            copies[0].wait_send()

            @pl.when(m // 2 != last_id // 2)
            def _():
                copies[1].wait_send()

        @pl.when(jnp.logical_not(first))
        def _():
            remote(dxbuf.at[m], gbuf.at[m], b_send.at[m], b_recv.at[m], me).wait_send()

            @pl.when(core == 0)
            def _():
                remote(dx0buf.at[m], dx0buf.at[m], r_send.at[m], d_recv.at[m], me).wait_send()

        @pl.when(first)
        def _():
            for k, dev in enumerate(dx0_dst):
                remote(dxbuf.at[m], dx0buf.at[m], d_send.at[m, k], d_recv.at[m], dev).wait_send()

        pltpu.make_async_copy(hbuf.at[m], hid_out.at[m], out_sem.at[0, m]).wait()
        pltpu.make_async_copy(xbuf.at[m], xs_out.at[m], out_sem.at[1, m]).wait()
        pltpu.make_async_copy(abuf.at[m], da_out.at[m], out_sem.at[2, m]).wait()
        pltpu.make_async_copy(gbuf.at[m], g_out.at[m], out_sem.at[3, m]).wait()
        pltpu.make_async_copy(dx0buf.at[m], dx0_out.at[m], out_sem.at[4, m]).wait()
        return carry

    lax.fori_loop(0, n_micro, drain, 0)
    for c in outs:
        c.wait()


class Plan:
    def __init__(self, vocab, n_stage):
        units = vocab // LANES
        self.base = units // 2 * LANES
        self.extra = vocab - 2 * self.base
        self.head_tile = next(t for t in (1600, 1536, 1280, 1024, 768, 640, 512, 256, 128) if self.base % t == 0)
        self.rows = 1024
        self.tiles = 9
        self.steps = 12
        arrive, self.before = 0.0, [0] * n_stage
        for s in reversed(range(n_stage)):
            self.before[s] = min(max(int((arrive - 4.5) / 2.6 + 0.3), 0), self.tiles)
            arrive += 2.3 if s % 2 else 4.6
        early = self.tiles * self.rows
        self.half_steps = self.steps // 2
        self.copy_rows = early // self.half_steps
        mid = self.base + self.extra
        self.spans = [(early, mid), (mid + early, vocab)]
        longest = max(b - a for a, b in self.spans)
        self.calc_rows = -(-longest // (16 * self.half_steps)) * 16
        self.over = [self.half_steps * self.calc_rows - (b - a) for a, b in self.spans]
        self.head = max(self.over)

    def calc_start(self, s):
        h, i = s // self.half_steps, s % self.half_steps
        return min(self.spans[h][0] + i * self.calc_rows, self.spans[h][1] - self.calc_rows)

    def copy_start(self, s):
        h, i = s // self.half_steps, s % self.half_steps
        return h * (self.base + self.extra) + i * self.copy_rows


def run_pipe(x0, emb, w_up, w_down, labels, n_stage, plan):
    n_micro, seq = labels.shape
    dim, ffn = w_up.shape
    n_tok = n_micro * seq
    base = plan.base
    e_parts = next(k for k in (10, 8, 5, 4, 2, 1) if base % (16 * k) == 0)
    any_spec = pl.BlockSpec(memory_space=pl.ANY)
    act = (n_micro, seq, dim)
    wide = (n_micro, seq, ffn)
    dma = pltpu.SemaphoreType.DMA
    vm = pltpu.VMEM
    pair = 2 * seq
    return pl.pallas_call(
        functools.partial(pipe_kernel, n_stage, plan),
        out_shape=[
            jax.ShapeDtypeStruct(act, BF16), jax.ShapeDtypeStruct(act, BF16), jax.ShapeDtypeStruct(wide, BF16),
            jax.ShapeDtypeStruct(wide, BF16), jax.ShapeDtypeStruct(act, BF16), jax.ShapeDtypeStruct(act, BF16),
            jax.ShapeDtypeStruct((n_stage, 8, pair), F32), jax.ShapeDtypeStruct((2, plan.tiles * plan.rows, dim), F32),
        ],
        in_specs=[any_spec] * 4 + [pl.BlockSpec(memory_space=pltpu.VMEM)],
        out_specs=[any_spec] * 8,
        scratch_shapes=[
            vm(act, BF16), vm(act, BF16), vm(wide, BF16), vm(wide, BF16), vm(act, BF16), vm(act, BF16), vm(act, BF16), vm(act, BF16), vm(act, BF16),
            vm((dim, ffn), BF16), vm((ffn, dim), BF16), vm((ffn, dim), BF16), vm((dim, ffn), BF16),
            vm((base + plan.extra, dim), BF16), vm((base + plan.extra, pair), BF16), vm((dim, pair), BF16), vm((pair, dim), F32),
            vm((seq, dim), F32), vm((seq, dim), F32), vm((seq, dim), BF16), vm((16, pair), F32), vm((16, pair), F32), vm((n_stage, 8, pair), F32),
            vm((2, 8, pair), F32), vm((dim, n_tok), BF16), vm((1, n_tok), F32), vm((plan.rows, n_tok), BF16), vm((2, plan.rows, dim), F32),
            dma((2,)), dma((e_parts + 1,)), dma((n_micro,)), dma((n_micro,)), dma((n_micro,)), dma((n_micro, 2)), dma((n_micro,)),
            dma((n_stage,)), dma((n_stage,)), dma((n_stage,)),
            dma((2,)), dma((2,)), dma, dma((n_stage,)), dma((n_stage,)), dma((n_stage,)),
            dma((n_micro,)), dma((n_micro,)), dma((n_micro, n_stage // 2)), dma((n_micro,)), dma((n_micro,)), dma((6, n_micro)),
            dma((2,)), dma((2,)), dma((plan.tiles,)), dma((plan.tiles,)),
        ],
        compiler_params=pltpu.CompilerParams(collective_id=0, has_side_effects=True, vmem_limit_bytes=67_000_000),
        cost_estimate=pl.CostEstimate(flops=60 * 10**9, bytes_accessed=100 * 10**6, transcendentals=0),
        name="pipe",
    )(x0, emb, w_up, w_down, labels.reshape(1, n_tok))


def fin_kernel(n_stage, n_tok, plan, cnt_ref, emb_hbm, tmp_hbm, n_hbm, stat_ref, lab_ref, rank_ref, sid_ref, dx0_hbm, xs_hbm, hid_hbm, da_hbm, g_hbm,
               out_hbm, loss_ref, gup_hbm, gdown_hbm,
               n_all, dx0, xs, hid, da, g, n_t, x_t, dx0s, dz, shift, e_in, c_out, cp, gup, gdown,
               ld_sem, e_sem, t_sem, co_sem, po_sem, gu_sem, gd_sem):
    dim = n_all.shape[1]
    ffn = da.shape[1]
    scale = dim ** -0.5
    inv_count = 1.0 / n_tok
    steps, half, crows, prows = plan.steps, plan.half_steps, plan.calc_rows, plan.copy_rows
    mid = plan.base + plan.extra
    wblk = 256
    n_wblk = ffn // wblk

    def calc_start(s):
        h, i = s // half, lax.rem(s, half)
        lo = jnp.where(h == 0, plan.spans[0][0], plan.spans[1][0]) + i * crows
        return pl.multiple_of(jnp.minimum(lo, jnp.where(h == 0, plan.spans[0][1], plan.spans[1][1]) - crows), 16)

    def copy_start(s):
        return pl.multiple_of(s // half * mid + lax.rem(s, half) * prows, 16)

    def e_copy(s):
        return pltpu.make_async_copy(emb_hbm.at[pl.ds(calc_start(s), crows)], e_in.at[lax.rem(s, 2)], e_sem.at[lax.rem(s, 2)])

    def t_copy(s):
        return pltpu.make_async_copy(tmp_hbm.at[pl.ds(pl.multiple_of(s * prows, 16), prows)], cp.at[lax.rem(s, 3)], t_sem.at[lax.rem(s, 3)])

    def p_out(s):
        return pltpu.make_async_copy(cp.at[lax.rem(s, 3)], out_hbm.at[pl.ds(copy_start(s), prows)], po_sem.at[lax.rem(s, 3)])

    def c_outs(s):
        slot = lax.rem(s, 2)
        start = calc_start(s)
        return (
            pltpu.make_async_copy(c_out.at[slot, pl.ds(plan.head, crows - plan.head)], out_hbm.at[pl.ds(start + plan.head, crows - plan.head)], co_sem.at[slot, 0]),
            pltpu.make_async_copy(c_out.at[slot, pl.ds(0, plan.head)], out_hbm.at[pl.ds(start, plan.head)], co_sem.at[slot, 1]),
        )

    def has_head(s):
        skip = False
        for h in range(2):
            if plan.over[h] > 0:
                skip = skip | (s == h * half + half - 1)
        return jnp.logical_not(skip)

    def c_start(s):
        a, b = c_outs(s)
        a.start()
        if plan.head:
            pl.when(has_head(s))(b.start)

    def c_wait(s):
        a, b = c_outs(s)
        a.wait()
        if plan.head:
            pl.when(has_head(s))(b.wait)

    loads = [pltpu.make_async_copy(s, d, ld_sem.at[i]) for i, (s, d) in enumerate(((n_hbm, n_all), (dx0_hbm, dx0), (xs_hbm, xs), (da_hbm, da), (hid_hbm, hid), (g_hbm, g)))]
    loads[0].start()
    loads[1].start()
    e_copy(0).start()
    t_copy(0).start()
    for c in loads[2:]:
        c.start()
    pair = stat_ref.shape[2]
    loss = jnp.zeros((1, pair), F32)
    for d in range(n_stage):
        if d % 2 == 0:
            shift[:, (d // 2) * pair:(d // 2 + 1) * pair] = stat_ref[d, 0:1, :] * LOG2E + math.log2(n_tok)
        loss = loss + stat_ref[d, 1:2, :]
    loss_ref[0] = jnp.sum(loss) * inv_count
    loads[0].wait()
    n_t[...] = n_all[...].T
    loads[1].wait()
    order = lax.broadcasted_iota(jnp.int32, (n_tok, n_tok), 0) == rank_ref[...]
    dx0s[...] = dot(jnp.where(order, 1.0, 0.0).astype(BF16), dx0[...]).astype(BF16)

    def rows_of(c, start, rows):
        hot = lax.broadcasted_iota(jnp.int32, (rows, LANES), 0) == sid_ref[pl.ds(c, 1), :] - start
        return dot(jnp.where(hot, 1.0, 0.0).astype(BF16), dx0s[pl.ds(pl.multiple_of(c * LANES, LANES), LANES), :])

    def first_blk(k):
        return jnp.minimum(cnt_ref[k] // LANES, n_tok // LANES - 1)

    def more(k, start, ref):
        def add(c, carry):
            ref[...] += rows_of(c, start, ref.shape[0])
            return carry

        lax.fori_loop(first_blk(k) + 1, (cnt_ref[k + 1] + LANES - 1) // LANES, add, 0)

    def step(s, carry):
        e_copy(s).wait()
        t_copy(s).wait()

        @pl.when(s + 1 < steps)
        def _():
            e_copy(s + 1).start()

            @pl.when(s >= 2)
            def _():
                p_out(s - 2).wait()

            t_copy(s + 1).start()

        @pl.when(s >= 2)
        def _():
            c_wait(s - 2)

        slot = lax.rem(s, 2)
        pslot = lax.rem(s, 3)
        start = calc_start(s)
        logit_grad(e_in[slot], n_t, shift, lab_ref, start, inv_count, scale, dz)
        c_out[slot] = dot(dz[...], n_all[...]) * scale + rows_of(first_blk(4 * s), start, crows)
        cp[pslot] += rows_of(first_blk(4 * s + 2), copy_start(s), prows)
        more(4 * s, start, c_out.at[slot])
        more(4 * s + 2, copy_start(s), cp.at[pslot])
        c_start(s)
        p_out(s).start()

        w = s - 2

        @pl.when(w == 0)
        def _():
            for c in loads[2:]:
                c.wait()
            x_t[...] = xs[...].T

        @pl.when((w >= 0) & (w < n_wblk))
        def _():
            cols = pl.ds(pl.multiple_of(w * wblk, wblk), wblk)
            wslot = lax.rem(w, 2)
            up_copy, down_copy = w_outs(w)

            @pl.when(w >= 2)
            def _():
                for c in w_outs(w - 2):
                    c.wait()

            gup[wslot] = dot(x_t[...], da[:, cols])
            gdown[wslot] = dot_t(hid[:, cols], g[...])
            up_copy.start()
            down_copy.start()

        return carry

    def w_outs(w):
        cols = pl.ds(pl.multiple_of(w * wblk, wblk), wblk)
        wslot = lax.rem(w, 2)
        return (pltpu.make_async_copy(gup.at[wslot], gup_hbm.at[:, cols], gu_sem.at[wslot]), pltpu.make_async_copy(gdown.at[wslot], gdown_hbm.at[cols], gd_sem.at[wslot]))

    lax.fori_loop(0, steps, step, 0)
    for w in range(n_wblk - 2, n_wblk):
        for c in w_outs(w):
            c.wait()
    for s in range(steps - 2, steps):
        c_wait(s)
    for s in range(steps - 3, steps):
        p_out(s).wait()


def run_fin(emb, tmp, n_all, stats, labels, rank, sid, cnt, dx0, xs, hid, da, g, n_stage, plan):
    vocab, dim = emb.shape
    n_tok, ffn = hid.shape
    vm = pltpu.VMEM
    dma = pltpu.SemaphoreType.DMA
    any_spec = pl.BlockSpec(memory_space=pl.ANY)
    vspec = pl.BlockSpec(memory_space=pltpu.VMEM)
    smem = pl.BlockSpec(memory_space=pltpu.SMEM)
    wblk = 256
    return pl.pallas_call(
        functools.partial(fin_kernel, n_stage, n_tok, plan),
        out_shape=[jax.ShapeDtypeStruct((vocab, dim), F32), jax.ShapeDtypeStruct((1,), F32), jax.ShapeDtypeStruct((dim, ffn), F32), jax.ShapeDtypeStruct((ffn, dim), F32)],
        in_specs=[smem, any_spec, any_spec, any_spec, vspec, vspec, vspec, vspec] + [any_spec] * 5,
        out_specs=[any_spec, smem, any_spec, any_spec],
        scratch_shapes=[
            vm((n_tok, dim), BF16), vm((n_tok, dim), BF16), vm((n_tok, dim), BF16), vm((n_tok, ffn), BF16), vm((n_tok, ffn), BF16), vm((n_tok, dim), BF16),
            vm((dim, n_tok), BF16), vm((dim, n_tok), BF16), vm((n_tok, dim), BF16), vm((plan.calc_rows, n_tok), BF16), vm((1, n_tok), F32),
            vm((2, plan.calc_rows, dim), BF16), vm((2, plan.calc_rows, dim), F32), vm((3, plan.copy_rows, dim), F32),
            vm((2, dim, wblk), F32), vm((2, wblk, dim), F32),
            dma((6,)), dma((2,)), dma((3,)), dma((2, 2)), dma((3,)), dma((2,)), dma((2,)),
        ],
        compiler_params=pltpu.CompilerParams(vmem_limit_bytes=67_000_000),
        cost_estimate=pl.CostEstimate(flops=2 * n_tok * vocab * dim, bytes_accessed=5 * vocab * dim, transcendentals=0),
        name="fin",
    )(cnt, emb, tmp, n_all, stats, labels.reshape(1, n_tok), rank, sid, dx0, xs, hid, da, g)


def solution(mesh):
    n_stage = mesh.shape["stage"]

    def device_fn(tokens, labels, emb, w_up, w_down):
        n_micro, seq = tokens.shape
        vocab, dim = emb.shape
        w_up, w_down = w_up[0], w_down[0]
        n_tok = n_micro * seq
        plan = Plan(vocab, n_stage)
        cuts = []
        for s in range(plan.steps):
            for lo, rows in ((plan.calc_start(s), plan.calc_rows), (plan.copy_start(s), plan.copy_rows)):
                cuts += [lo, lo + rows]
        cuts = jnp.array(cuts + [vocab] * (LANES - len(cuts)), jnp.int32).reshape(1, LANES)
        x0, rank, sid, cnt = run_gather(tokens, emb, cuts, n_stage)
        n_all, xs, hid, da, g, dx0, stats, tmp = run_pipe(x0, emb, w_up, w_down, labels, n_stage, plan)
        flat = lambda p: p.reshape(n_tok, -1)
        grad_emb, loss, grad_up, grad_down = run_fin(
            emb, tmp.reshape(-1, dim), flat(n_all), stats, labels, rank, sid, cnt.reshape(LANES), flat(dx0), flat(xs), flat(hid), flat(da), flat(g), n_stage, plan
        )
        return loss, grad_up[None], grad_down[None], grad_emb

    return jax.shard_map(device_fn, mesh=mesh, in_specs=(P("dp", None), P("dp", None), P(None, None), P("stage", None, None), P("stage", None, None)), out_specs=(P("dp"), P(("dp", "stage"), None, None), P(("dp", "stage"), None, None), P("dp", None)), check_vma=False)
```

time: 259 us -> 200 us (0.77)
  Pallas kernels: 225 us -> 195 us
  matrix products: 11.5 us -> 0 us
  local copies, waits for them, and re-layouts: 14.2 us -> 3.73 us
  other arithmetic: 7.35 us -> 0 us
    pallas_call x2 -> x3, Pallas kernels: 225 us -> 195 us  [the longest x1 128 us: run_pipe(): pl.pallas_call(functools.partial(pipe_kernel, n_stage, plan), out_shape=[...]
    gather x1 -> x0, local copies, waits for them, and re-layouts: 13 us -> none  [device_fn(): x0 = jnp.take(emb, flat, axis=0).reshape(n_micro, seq, dim)]
    dot_general x2 -> x0, matrix products: 11.5 us -> none  [device_fn(): lax.dot_general(p.reshape(n_tok, -1), q.reshape(n_tok, -1), (((0,), (0,))...]
    reduce_sum x3 -> x0, other arithmetic: 4.78 us -> none  [the longest x1 1.78 us: run_emb(): sid = jnp.sum(jnp.where(rank[None, :] == pos[:, None], tr, 0), axis=1)]
    unnamed x6 -> x12, local copies, waits for them, and re-layouts: 0.01 us -> 3.73 us
where the time goes in v2:
time: 200 us; the launch traced here: 199 us
  Pallas kernels  195 us (98%)
  local copies, waits for them, and re-layouts  3.73 us (2%)
    pallas_call x1, Pallas kernels, run_pipe(): pl.pallas_call(functools.partial(pipe_kernel, n_stage, plan), out_shape=[...  128 us
    pallas_call x1, Pallas kernels, run_fin(): pl.pallas_call(functools.partial(fin_kernel, n_stage, n_tok, plan), out_s...  63.2 us

profile of v2, /device:TPU:125, one launch (start us, length us, event | category | flops | bytes accessed | tf_op | source)
XLA Modules:
  0.0 199.4 jit_solution(12764190714508108270)
XLA Ops:
  0.6 0.0 copy-start
  0.6 0.7 copy-done
  1.3 0.0 copy-start.1
  1.3 0.7 copy-done.1
  2.0 3.4 %gather.1 = (bf16[2,128,512]{2,1,0:T(8,128)(2,1)S(1)}, s32[1,1024]{1,0:T(1,128)S(1)}, s32[8,128]{1,0:T(8,128)S(1)}, s32[1,128]{1,0:T(1,128)S(1)}) custom-call(s32[1024]{0:T(1024)S(1)} %bitcast.15, s32[1,1024]{1,0:T(1,128)S(1)} %bitcast.16, s32[8,128]{1,0:T(8,128)S(1)} %copy-done, s32[1,128]{1,0:T(1,128)S(1)} %copy-done.1, bf16[32128,512]{1,0:T(8,128)(2,1)} %emb_hbm.5), custom_call_target="tpu_custom_call" | custom-call | flops 1000000000 | bytes 4194304 | tf_op jit(solution)/shard_map/gather/pallas_call | solution.py:118
  5.4 0.0 copy-start.2
  5.4 0.7 copy-done.2
  6.1 0.0 copy-start.3
  6.1 0.6 copy-done.3
  6.7 0.0 copy-start.4
  6.7 0.6 copy-done.4
  7.3 0.0 copy-start.5
  7.3 0.5 copy-done.5
  7.8 128.3 %pipe.1 = (bf16[8,128,512]{2,1,0:T(8,128)(2,1)}, bf16[8,128,512]{2,1,0:T(8,128)(2,1)}, bf16[8,128,2048]{2,1,0:T(8,128)(2,1)}, bf16[8,128,2048]{2,1,0:T(8,128)(2,...) custom-call(bf16[2,128,512]{2,1,0:T(8,128)(2,1)} %copy-done.2, ...), custom_call_target="tpu_custom_call" | custom-call | flops 60000002048 | bytes 100000000 | tf_op jit(solution)/shard_map/pipe/pallas_call | solution.py:584
  136.1 63.2 %fin.1 = (f32[32128,512]{1,0:T(8,128)}, f32[1]{0:T(128)}, f32[512,2048]{1,0:T(8,128)}, f32[2048,512]{1,0:T(8,128)}) custom-call(s32[128]{0:T(128)} %bitcast.17, bf16[32128,512]{1,0:T(8,128)(2,1)} %emb_hbm.5, f32[18432,512]{1,0:T(8,128)} %bitcast.22, bf16[1024,512]{1,0:T(8,128)(2,1)} %bitcast.27, f32[8,8,256]{2,1,0:T(8,128)} %get-tuple-element.24.stat_ref, ...), custom_call_target="tpu_custom_call" | custom-call | flops 33688649728 | bytes 82247680 | tf_op jit(solution)/shard_map/fin/pallas_call | solution.py:781
Async XLA Ops:
  0.6 0.7 copy-start
  1.3 0.7 copy-start.1
  5.4 0.7 copy-start.2
  6.1 0.6 copy-start.3
  6.7 0.6 copy-start.4
  7.3 0.5 copy-start.5

commit v3 on v2

--- a/solution.py
+++ b/solution.py
@@ -41,9 +41,12 @@
     return pltpu.make_async_remote_copy(src_ref=src, dst_ref=dst, send_sem=send_sem, recv_sem=recv_sem, device_id={"stage": dev}, device_id_type=MESH)
 
 
-def gather_kernel(n_stage, ids_ref, row_ref, tok_ref, cut_ref, emb_hbm, x0_out, rank_out, sid_out, cnt_out, tiles, sem):
+def column(row):
+    return jnp.broadcast_to(row, (LANES, LANES)).T
+
+
+def gather_kernel(ids_ref, tok_ref, emb_hbm, x0_hbm, tiles, picked, sem, out_sem):
     n_micro, seq = tok_ref.shape
-    n_tok = n_micro * seq
     me = lax.axis_index("stage")
     group = tiles.shape[1] // seq
     slots = tiles.shape[0]
@@ -58,76 +61,80 @@
 
         lax.fori_loop(0, seq, one, 0, unroll=8)
 
-    fetch(0)
-    for k in range(1, slots):
-        pl.when(me < slots)(functools.partial(fetch, k))
-
-    def column(row):
-        return jnp.broadcast_to(row, (LANES, LANES)).T
-
+    def select(k):
+        sub = lax.broadcasted_iota(jnp.int32, (LANES, LANES), 0)
+        lane = lax.broadcasted_iota(jnp.int32, (LANES, LANES), 1)
+        tok = column(tok_ref[pl.ds(owners[k], 1), :].astype(F32)).astype(jnp.int32)
+        want = sub * group + (tok - tok // group * group)
+        hot = jnp.concatenate([jnp.where(lane + b * LANES == want, 1.0, 0.0).astype(BF16) for b in range(seq * group // LANES)], axis=1)
+        pltpu.make_async_copy(emb_hbm.at[pl.ds(0, seq * group)], tiles.at[k], sem.at[k]).wait()
+        picked[k] = dot(hot, tiles[k]).astype(BF16)
+        pltpu.make_async_copy(picked.at[k], x0_hbm.at[k], out_sem.at[k]).start()
+
+    def finish(k):
+        pltpu.make_async_copy(picked.at[k], x0_hbm.at[k], out_sem.at[k]).wait()
+
+    for work in (fetch, select, finish):
+        work(0)
+        for k in range(1, slots):
+            pl.when(me < slots)(functools.partial(work, k))
+
+
+def head_chunk(dev, k, n_micro):
+    return jnp.minimum(jnp.where(dev < 2, 2 * dev + k, dev + 2), n_micro - 1)
+
+
+def run_gather(tokens, emb):
+    n_micro, seq = tokens.shape
+    dim = emb.shape[1]
+    group = 16
+    return pl.pallas_call(
+        gather_kernel,
+        out_shape=jax.ShapeDtypeStruct((2, seq, dim), BF16),
+        in_specs=[pl.BlockSpec(memory_space=pltpu.SMEM), pl.BlockSpec(memory_space=pltpu.VMEM), pl.BlockSpec(memory_space=pl.ANY)],
+        out_specs=pl.BlockSpec(memory_space=pl.ANY),
+        scratch_shapes=[pltpu.VMEM((2, seq * group, dim), BF16), pltpu.VMEM((2, seq, dim), BF16), pltpu.SemaphoreType.DMA((2,)), pltpu.SemaphoreType.DMA((2,))],
+        cost_estimate=pl.CostEstimate(flops=10**9, bytes_accessed=2 * seq * group * dim * 2, transcendentals=0),
+        name="gather",
+    )(tokens.reshape(n_micro * seq), tokens, emb)
+
+
+def token_table(row_ref, cut_ref, meta):
+    n_tok = row_ref.shape[1]
+    n_grp = n_tok // LANES
+    lane = lax.broadcasted_iota(jnp.int32, (LANES, LANES), 1).astype(F32)
     sub = lax.broadcasted_iota(jnp.int32, (LANES, LANES), 0)
-    lane = lax.broadcasted_iota(jnp.int32, (LANES, LANES), 1)
-    tok_row = row_ref[...]
-    key_row = tok_row * n_tok + lax.broadcasted_iota(jnp.int32, (1, n_tok), 1)
-    n_grp = n_tok // LANES
-    cols = [column(tok_row[:, c * LANES:(c + 1) * LANES].astype(F32)) for c in range(n_grp)]
-    keys = [cols[c].astype(jnp.int32) * n_tok + (sub + c * LANES) for c in range(n_grp)]
+    row = lambda g: row_ref[:, g * LANES:(g + 1) * LANES].astype(F32)
+    zero = jnp.zeros((LANES, LANES), F32)
+    fold = lambda acc: jnp.sum(acc, axis=0, keepdims=True)
+    cols = [column(row(c)) for c in range(n_grp)]
+    firsts = []
+    for g in range(n_grp):
+        acc = zero
+        for c in range(g + 1):
+            same = cols[c] == row(g)
+            if c == g:
+                same = same & (sub < lane.astype(jnp.int32))
+            acc = acc + jnp.where(same, 1.0, 0.0)
+        firsts.append(column(jnp.where(fold(acc) == 0.0, 1.0, 0.0)))
     ranks = []
     for g in range(n_grp):
-        mine = key_row[:, g * LANES:(g + 1) * LANES]
-        acc = jnp.zeros((LANES, LANES), F32)
+        acc = zero
         for c in range(n_grp):
-            acc = acc + jnp.where(keys[c] < mine, 1.0, 0.0)
-        ranks.append(jnp.sum(acc, axis=0, keepdims=True))
-        rank_out[:, g * LANES:(g + 1) * LANES] = ranks[g].astype(jnp.int32)
+            acc = acc + jnp.where(cols[c] < row(g), firsts[c], 0.0)
+        ranks.append(fold(acc))
+        meta[g:g + 1, :] = ranks[g].astype(jnp.int32)
     rank_cols = [column(r) for r in ranks]
     for g in range(n_grp):
-        want = (lane + g * LANES).astype(F32)
-        acc = jnp.zeros((LANES, LANES), F32)
+        acc = zero
         for c in range(n_grp):
-            acc = acc + jnp.where(rank_cols[c] == want, cols[c], 0.0)
-        sid_out[g:g + 1, :] = jnp.sum(acc, axis=0, keepdims=True).astype(jnp.int32)
+            acc = acc + jnp.where(rank_cols[c] == lane + g * LANES, firsts[c] * cols[c], 0.0)
+        meta[n_grp + g:n_grp + g + 1, :] = fold(acc).astype(jnp.int32)
     cut = cut_ref[...].astype(F32)
-    acc = jnp.zeros((LANES, LANES), F32)
+    acc = zero
     for c in range(n_grp):
-        acc = acc + jnp.where(cols[c] < cut, 1.0, 0.0)
-    cnt_out[...] = jnp.sum(acc, axis=0, keepdims=True).astype(jnp.int32)
-
-    def select(k):
-        pltpu.make_async_copy(emb_hbm.at[pl.ds(0, seq * group)], tiles.at[k], sem.at[k]).wait()
-        tok = column(tok_ref[pl.ds(owners[k], 1), :].astype(F32)).astype(jnp.int32)
-        want = sub * group + (tok - tok // group * group)
-        hot = [jnp.where(lane + b * LANES == want, 1.0, 0.0).astype(BF16) for b in range(seq * group // LANES)]
-        x0_out[k] = dot(jnp.concatenate(hot, axis=1), tiles[k]).astype(BF16)
-
-    select(0)
-    for k in range(1, slots):
-        pl.when(me < slots)(functools.partial(select, k))
-
-
-def head_chunk(dev, k, n_micro):
-    return jnp.minimum(jnp.where(dev < 2, 2 * dev + k, dev + 2), n_micro - 1)
-
-
-def run_gather(tokens, emb, cuts, n_stage):
-    n_micro, seq = tokens.shape
-    n_tok = n_micro * seq
-    dim = emb.shape[1]
-    group = 16
-    vspec = pl.BlockSpec(memory_space=pltpu.VMEM)
-    return pl.pallas_call(
-        functools.partial(gather_kernel, n_stage),
-        out_shape=[
-            jax.ShapeDtypeStruct((2, seq, dim), BF16), jax.ShapeDtypeStruct((1, n_tok), jnp.int32),
-            jax.ShapeDtypeStruct((n_tok // LANES, LANES), jnp.int32), jax.ShapeDtypeStruct((1, LANES), jnp.int32),
-        ],
-        in_specs=[pl.BlockSpec(memory_space=pltpu.SMEM), vspec, vspec, vspec, pl.BlockSpec(memory_space=pl.ANY)],
-        out_specs=[vspec] * 4,
-        scratch_shapes=[pltpu.VMEM((2, seq * group, dim), BF16), pltpu.SemaphoreType.DMA((2,))],
-        compiler_params=pltpu.CompilerParams(vmem_limit_bytes=32 * 1000 * 1000),
-        cost_estimate=pl.CostEstimate(flops=10**9, bytes_accessed=2 * seq * group * dim * 2, transcendentals=0),
-        name="gather",
-    )(tokens.reshape(n_tok), tokens.reshape(1, n_tok), tokens, cuts, emb)
+        acc = acc + jnp.where(cols[c] < cut, firsts[c], 0.0)
+    meta[2 * n_grp:3 * n_grp, :] = jnp.broadcast_to(fold(acc), (n_grp, LANES)).astype(jnp.int32)
 
 
 def logit_grad(e, n_t, shift, lab, first_id, inv_count, scale, dz):
@@ -142,12 +149,12 @@
         dz[:, cols] = jnp.where(vid == lab[:, cols] - first_id, prob - inv_count, prob).astype(BF16)
 
 
-def pipe_kernel(n_stage, plan, x0_hbm, emb_hbm, up_hbm, down_hbm, lab_ref,
-                n_out, xs_out, hid_out, da_out, g_out, dx0_out, stat_out, tmp_out,
+def pipe_kernel(n_stage, plan, x0_hbm, emb_hbm, up_hbm, down_hbm, lab_ref, row_ref, cut_ref,
+                n_out, xs_out, hid_out, da_out, g_out, dx0_out, stat_out, tmp_out, meta_out,
                 xbuf, ybuf, abuf, hbuf, nbuf, gbuf, dxbuf, dx0buf, dnbuf, up, down, up_t, down_t,
-                emb, zbuf, n_t, dn_acc, dn_send, dn_recv, dn_own, st_send, st_recv, statall, tops, n_all_t, shift, dz, obuf,
+                emb, zbuf, n_t, dn_acc, dn_send, dn_recv, dn_own, st_send, st_recv, statall, tops, n_all_t, shift, dz, obuf, z_pair, meta,
                 w_sem, e_sem, x_sem, f_send, f_recv, n_send, n_recv, ag_send, ag_recv, fw_send,
-                st_sems, dp_sems, dn_ssem, dn_rsem, sa_send, sa_recv, b_send, b_recv, d_send, d_recv, r_send, out_sem, x_send, o_sem, od_send, od_recv):
+                st_sems, dp_sems, dn_ssem, dn_rsem, sa_send, sa_recv, b_send, b_recv, d_send, d_recv, r_send, rf_send, out_sem, x_send, o_sem, od_send, od_recv):
     n_micro, seq, dim = xbuf.shape
     n_tok = n_micro * seq
     ffn = up.shape[1]
@@ -187,24 +194,24 @@
         return pltpu.make_async_copy(src, emb.at[pl.ds(i * e_step, e_step)], e_sem.at[i])
 
     e_more = pltpu.make_async_copy(emb_hbm.at[pl.ds(base, extra)], emb.at[pl.ds(base, extra)], e_sem.at[e_parts])
+    pl.semaphore_wait(barrier, n_stage - 1)
+
+    def x_copy(k):
+        return remote(x0_hbm.at[k], xbuf.at[x_mine[k]], x_send.at[k], f_recv.at[x_mine[k]], 0)
+
+    @pl.when(jnp.logical_not(first) & (me + 2 < n_micro))
+    def _():
+        x_copy(0).start()
+
+        @pl.when(me < 2)
+        def _():
+            x_copy(1).start()
+
+    for c in w_copy:
+        c.wait()
     for i in range(e_parts):
         e_copy(i).start()
     pl.when(core == 0)(e_more.start)
-    pl.semaphore_wait(barrier, n_stage - 1)
-
-    def x_copy(k):
-        return remote(x0_hbm.at[k], xbuf.at[x_mine[k]], x_send.at[k], f_recv.at[x_mine[k]], 0)
-
-    @pl.when(jnp.logical_not(first) & (me + 2 < n_micro))
-    def _():
-        x_copy(0).start()
-
-        @pl.when(me < 2)
-        def _():
-            x_copy(1).start()
-
-    for c in w_copy:
-        c.wait()
 
     def transpose_weights():
         for j in range(n_fblk):
@@ -288,22 +295,45 @@
     log_count = math.log2(n_tok)
     lab = lab_ref[:, pl.ds(pl.multiple_of(chip * pair, pair), pair)]
 
-    def logits(rows, size, top, tot):
-        z = (dot(emb[rows, :], n_t[...]) * scale).astype(BF16)
+    def logits(rows, size):
+        e = emb[rows, :]
+        parts = [dot(e[k * size // 2:(k + 1) * size // 2], n_t[...]) for k in range(2)]
+        z = jnp.concatenate([(p * scale).astype(BF16) for p in parts], axis=0)
         zbuf[rows, :] = z
-        z3 = z.astype(F32).reshape(size // 8, 8, pair)
-        new_top = jnp.maximum(top, jnp.max(z3, axis=0))
-        off = new_top * LOG2E
-        return new_top, tot * jnp.exp2(top * LOG2E - off) + jnp.sum(jnp.exp2(z3 * LOG2E - off[None]), axis=0)
+        return z
+
+    def peak(z, size, top):
+        best = jnp.max(z.reshape(size // 16, 16, pair), axis=0).astype(F32)
+        return jnp.maximum(top, jnp.maximum(best[:8], best[8:]))
+
+    def total(z, size, old, top, tot):
+        off = top * LOG2E
+        return tot * jnp.exp2(old * LOG2E - off) + jnp.sum(jnp.exp2(z.astype(F32).reshape(size // 8, 8, pair) * LOG2E - off[None]), axis=0)
 
     tops[0] = jnp.full((8, pair), -jnp.inf, F32)
     tops[1] = jnp.zeros((8, pair), F32)
 
     @pl.when(core == 0)
     def _():
-        tops[0], tops[1] = logits(pl.ds(base, extra), extra, tops[0], tops[1])
-
-    top, tot = lax.fori_loop(0, n_tiles, lambda i, c: logits(pl.ds(pl.multiple_of(i * tile, 16), tile), tile, *c), (tops[0], tops[1]))
+        z = logits(pl.ds(base, extra), extra)
+        top = peak(z, extra, tops[0])
+        tops[1] = total(z, extra, tops[0], top, tops[1])
+        tops[0] = top
+
+    def logits_step(i, slot, old, top, tot):
+        z = logits(pl.ds(pl.multiple_of(i * tile, 16), tile), tile)
+        tot = total(z_pair[1 - slot], tile, old, top, tot)
+        z_pair[slot] = z
+        return top, peak(z, tile, top), tot
+
+    z = logits(pl.ds(0, tile), tile)
+    z_pair[0] = z
+    state = (tops[0], peak(z, tile, tops[0]), tops[1])
+    state = lax.fori_loop(0, (n_tiles - 1) // 2, lambda i, c: logits_step(2 * i + 2, 0, *logits_step(2 * i + 1, 1, *c)), state)
+    if n_tiles % 2 == 0:
+        state = logits_step(n_tiles - 1, 1, *state)
+    old, top, tot = state
+    tot = total(z_pair[(n_tiles - 1) % 2], tile, old, top, tot)
     row_top = jnp.max(top, axis=0, keepdims=True)
     row_tot = jnp.sum(tot * jnp.exp2((top - row_top) * LOG2E), axis=0, keepdims=True)
     st_send[0:8, :] = jnp.broadcast_to(row_top, (8, pair))
@@ -369,7 +399,16 @@
         pl.when(jnp.logical_not(last))(got.wait_recv)
         pl.when(mate != last_id)(remote(nbuf.at[p], nbuf.at[p], fw_send.at[p], ag_recv.at[p], mate).start)
 
-    dx0_dst = [1] + list(range(2, n_stage, 2))
+    near_dst = [1, 2, n_stage - 2]
+    far_dst = n_stage // 2
+    n_relay = (n_micro - 2) // 2
+
+    def dx0_copies(m):
+        return [remote(dxbuf.at[m], dx0buf.at[m], d_send.at[m, k], d_recv.at[m], dev) for k, dev in enumerate(near_dst + [far_dst])]
+
+    def relay_far(j):
+        m = 2 * j + jnp.where(me == 2, 0, 1)
+        return remote(dx0buf.at[m], dx0buf.at[m], rf_send.at[j], d_recv.at[m], far_dst)
 
     def bwd(m):
         @pl.when(jnp.logical_not(last))
@@ -401,8 +440,10 @@
 
         @pl.when(first)
         def _():
-            for k, dev in enumerate(dx0_dst):
-                remote(dxbuf.at[m], dx0buf.at[m], d_send.at[m, k], d_recv.at[m], dev).start()
+            copies = dx0_copies(m)
+            for c in copies[:-1]:
+                c.start()
+            pl.when(m >= 2 * n_relay)(copies[-1].start)
 
         pltpu.make_async_copy(abuf.at[m], da_out.at[m], out_sem.at[2, m]).start()
         pltpu.make_async_copy(gbuf.at[m], g_out.at[m], out_sem.at[3, m]).start()
@@ -421,6 +462,7 @@
             for d in range(1, n_stage // 2):
                 src = lax.rem(mate + 2 * d, n_stage)
                 pl.when(jnp.logical_not(last))(remote(nbuf.at[src], nbuf.at[src], ag_send.at[0], ag_recv.at[src], me).wait_recv)
+            token_table(row_ref, cut_ref, meta)
             for m in range(n_micro):
                 n_all_t[:, m * seq:(m + 1) * seq] = nbuf[m].T
             for c in range(n_stage // 2):
@@ -441,23 +483,33 @@
         own.start()
         far_copy.start()
 
+    relays = (me == 2) | (me == n_stage - 2)
     before = sum(jnp.where(me == s, plan.before[s], 0) for s in range(n_stage))
 
     def work(i, carry):
         chunk = (i >= before) & (i < before + n_micro)
         pl.when(chunk)(lambda: bwd(i - before))
         pl.when(jnp.logical_not(chunk))(lambda: emb_tile(jnp.where(i < before, i, i - n_micro)))
+        j = i - n_micro - jnp.where(me == 2, before, plan.tiles - n_relay)
+
+        @pl.when(relays & (j >= 0) & (j < n_relay))
+        def _():
+            copy = relay_far(j)
+            copy.wait_recv()
+            copy.start()
+
         return carry
 
     lax.fori_loop(0, plan.tiles + n_micro, work, 0)
-    outs = [pltpu.make_async_copy(nbuf, n_out, out_sem.at[5, 0]), pltpu.make_async_copy(statall, stat_out, out_sem.at[5, 1])]
+    outs = [pltpu.make_async_copy(nbuf, n_out, out_sem.at[5, 0]), pltpu.make_async_copy(statall, stat_out, out_sem.at[5, 1]), pltpu.make_async_copy(meta, meta_out, out_sem.at[5, 2])]
     for c in outs:
         c.start()
 
     def relay(m, carry):
         @pl.when(jnp.logical_not(first))
         def _():
-            remote(dx0buf.at[m], dx0buf.at[m], r_send.at[m], d_recv.at[m], me).wait_recv()
+            relayed = relays & (m < 2 * n_relay) & (lax.rem(m, 2) == jnp.where(me == 2, 0, 1))
+            pl.when(jnp.logical_not(relayed))(remote(dx0buf.at[m], dx0buf.at[m], r_send.at[m], d_recv.at[m], me).wait_recv)
 
             @pl.when(core == 0)
             def _():
@@ -480,6 +532,8 @@
     for k in range(plan.tiles):
         rows = pl.ds(k * plan.rows, plan.rows)
         remote(obuf.at[0], tmp_out.at[1 - core, rows], od_send.at[k], od_recv.at[k], me).wait_recv()
+    for j in range(n_relay):
+        pl.when(relays)(relay_far(j).wait_send)
     for c in sa_copies:
         c.wait_send()
     for c, p in zip(ag_copies, peers):
@@ -522,8 +576,10 @@
 
         @pl.when(first)
         def _():
-            for k, dev in enumerate(dx0_dst):
-                remote(dxbuf.at[m], dx0buf.at[m], d_send.at[m, k], d_recv.at[m], dev).wait_send()
+            copies = dx0_copies(m)
+            for c in copies[:-1]:
+                c.wait_send()
+            pl.when(m >= 2 * n_relay)(copies[-1].wait_send)
 
         pltpu.make_async_copy(hbuf.at[m], hid_out.at[m], out_sem.at[0, m]).wait()
         pltpu.make_async_copy(xbuf.at[m], xs_out.at[m], out_sem.at[1, m]).wait()
@@ -569,7 +625,7 @@
         return h * (self.base + self.extra) + i * self.copy_rows
 
 
-def run_pipe(x0, emb, w_up, w_down, labels, n_stage, plan):
+def run_pipe(x0, emb, w_up, w_down, labels, tokens, cuts, n_stage, plan):
     n_micro, seq = labels.shape
     dim, ffn = w_up.shape
     n_tok = n_micro * seq
@@ -587,28 +643,30 @@
             jax.ShapeDtypeStruct(act, BF16), jax.ShapeDtypeStruct(act, BF16), jax.ShapeDtypeStruct(wide, BF16),
             jax.ShapeDtypeStruct(wide, BF16), jax.ShapeDtypeStruct(act, BF16), jax.ShapeDtypeStruct(act, BF16),
             jax.ShapeDtypeStruct((n_stage, 8, pair), F32), jax.ShapeDtypeStruct((2, plan.tiles * plan.rows, dim), F32),
+            jax.ShapeDtypeStruct((3 * n_tok // LANES, LANES), jnp.int32),
         ],
-        in_specs=[any_spec] * 4 + [pl.BlockSpec(memory_space=pltpu.VMEM)],
-        out_specs=[any_spec] * 8,
+        in_specs=[any_spec] * 4 + [pl.BlockSpec(memory_space=pltpu.VMEM)] * 3,
+        out_specs=[any_spec] * 9,
         scratch_shapes=[
             vm(act, BF16), vm(act, BF16), vm(wide, BF16), vm(wide, BF16), vm(act, BF16), vm(act, BF16), vm(act, BF16), vm(act, BF16), vm(act, BF16),
             vm((dim, ffn), BF16), vm((ffn, dim), BF16), vm((ffn, dim), BF16), vm((dim, ffn), BF16),
             vm((base + plan.extra, dim), BF16), vm((base + plan.extra, pair), BF16), vm((dim, pair), BF16), vm((pair, dim), F32),
             vm((seq, dim), F32), vm((seq, dim), F32), vm((seq, dim), BF16), vm((16, pair), F32), vm((16, pair), F32), vm((n_stage, 8, pair), F32),
             vm((2, 8, pair), F32), vm((dim, n_tok), BF16), vm((1, n_tok), F32), vm((plan.rows, n_tok), BF16), vm((2, plan.rows, dim), F32),
+            vm((2, plan.head_tile, pair), BF16), vm((3 * n_tok // LANES, LANES), jnp.int32),
             dma((2,)), dma((e_parts + 1,)), dma((n_micro,)), dma((n_micro,)), dma((n_micro,)), dma((n_micro, 2)), dma((n_micro,)),
             dma((n_stage,)), dma((n_stage,)), dma((n_stage,)),
             dma((2,)), dma((2,)), dma, dma((n_stage,)), dma((n_stage,)), dma((n_stage,)),
-            dma((n_micro,)), dma((n_micro,)), dma((n_micro, n_stage // 2)), dma((n_micro,)), dma((n_micro,)), dma((6, n_micro)),
+            dma((n_micro,)), dma((n_micro,)), dma((n_micro, 4)), dma((n_micro,)), dma((n_micro,)), dma((n_micro,)), dma((6, n_micro)),
             dma((2,)), dma((2,)), dma((plan.tiles,)), dma((plan.tiles,)),
         ],
         compiler_params=pltpu.CompilerParams(collective_id=0, has_side_effects=True, vmem_limit_bytes=67_000_000),
         cost_estimate=pl.CostEstimate(flops=60 * 10**9, bytes_accessed=100 * 10**6, transcendentals=0),
         name="pipe",
-    )(x0, emb, w_up, w_down, labels.reshape(1, n_tok))
-
-
-def fin_kernel(n_stage, n_tok, plan, cnt_ref, emb_hbm, tmp_hbm, n_hbm, stat_ref, lab_ref, rank_ref, sid_ref, dx0_hbm, xs_hbm, hid_hbm, da_hbm, g_hbm,
+    )(x0, emb, w_up, w_down, labels.reshape(1, n_tok), tokens.reshape(1, n_tok), cuts)
+
+
+def fin_kernel(n_stage, n_tok, plan, ids_ref, emb_hbm, tmp_hbm, n_hbm, stat_ref, lab_ref, meta_ref, dx0_hbm, xs_hbm, hid_hbm, da_hbm, g_hbm,
                out_hbm, loss_ref, gup_hbm, gdown_hbm,
                n_all, dx0, xs, hid, da, g, n_t, x_t, dx0s, dz, shift, e_in, c_out, cp, gup, gdown,
                ld_sem, e_sem, t_sem, co_sem, po_sem, gu_sem, gd_sem):
@@ -682,22 +740,31 @@
     loads[0].wait()
     n_t[...] = n_all[...].T
     loads[1].wait()
-    order = lax.broadcasted_iota(jnp.int32, (n_tok, n_tok), 0) == rank_ref[...]
-    dx0s[...] = dot(jnp.where(order, 1.0, 0.0).astype(BF16), dx0[...]).astype(BF16)
-
-    def rows_of(c, start, rows):
-        hot = lax.broadcasted_iota(jnp.int32, (rows, LANES), 0) == sid_ref[pl.ds(c, 1), :] - start
-        return dot(jnp.where(hot, 1.0, 0.0).astype(BF16), dx0s[pl.ds(pl.multiple_of(c * LANES, LANES), LANES), :])
-
-    def first_blk(k):
-        return jnp.minimum(cnt_ref[k] // LANES, n_tok // LANES - 1)
-
-    def more(k, start, ref):
-        def add(c, carry):
-            ref[...] += rows_of(c, start, ref.shape[0])
+    dense = jnp.concatenate([meta_ref[g:g + 1, :] for g in range(n_tok // LANES)], axis=1)
+    order = lax.broadcasted_iota(jnp.int32, (n_tok, n_tok), 0) == dense
+    dx0s[...] = dot(jnp.where(order, 1.0, 0.0).astype(BF16), dx0[...])
+
+    def add_rows(k, start, ref):
+        lo, hi = ids_ref[2 * n_tok + k], ids_ref[2 * n_tok + k + 1]
+        wide = 8
+
+        def some(p, width):
+            at = [pl.ds(ids_ref[n_tok + p + u] - start, 1) for u in range(width)]
+            new = [ref[at[u], :] + dx0s[pl.ds(p + u, 1), :] for u in range(width)]
+            for u in range(width):
+                ref[at[u], :] = new[u]
+
+        def group(g, carry):
+            some(lo + g * wide, wide)
             return carry
 
-        lax.fori_loop(first_blk(k) + 1, (cnt_ref[k + 1] + LANES - 1) // LANES, add, 0)
+        def single(p, carry):
+            some(p, 1)
+            return carry
+
+        n_grp = (hi - lo) // wide
+        lax.fori_loop(0, n_grp, group, 0)
+        lax.fori_loop(lo + n_grp * wide, hi, single, 0)
 
     def step(s, carry):
         e_copy(s).wait()
@@ -720,13 +787,12 @@
         slot = lax.rem(s, 2)
         pslot = lax.rem(s, 3)
         start = calc_start(s)
+        add_rows(4 * s + 2, copy_start(s), cp.at[pslot])
+        p_out(s).start()
         logit_grad(e_in[slot], n_t, shift, lab_ref, start, inv_count, scale, dz)
-        c_out[slot] = dot(dz[...], n_all[...]) * scale + rows_of(first_blk(4 * s), start, crows)
-        cp[pslot] += rows_of(first_blk(4 * s + 2), copy_start(s), prows)
-        more(4 * s, start, c_out.at[slot])
-        more(4 * s + 2, copy_start(s), cp.at[pslot])
+        c_out[slot] = dot(dz[...], n_all[...]) * scale
+        add_rows(4 * s, start, c_out.at[slot])
         c_start(s)
-        p_out(s).start()
 
         w = s - 2
 
@@ -769,7 +835,7 @@
         p_out(s).wait()
 
 
-def run_fin(emb, tmp, n_all, stats, labels, rank, sid, cnt, dx0, xs, hid, da, g, n_stage, plan):
+def run_fin(emb, tmp, n_all, stats, labels, meta, dx0, xs, hid, da, g, n_stage, plan):
     vocab, dim = emb.shape
     n_tok, ffn = hid.shape
     vm = pltpu.VMEM
@@ -781,11 +847,11 @@
     return pl.pallas_call(
         functools.partial(fin_kernel, n_stage, n_tok, plan),
         out_shape=[jax.ShapeDtypeStruct((vocab, dim), F32), jax.ShapeDtypeStruct((1,), F32), jax.ShapeDtypeStruct((dim, ffn), F32), jax.ShapeDtypeStruct((ffn, dim), F32)],
-        in_specs=[smem, any_spec, any_spec, any_spec, vspec, vspec, vspec, vspec] + [any_spec] * 5,
+        in_specs=[smem, any_spec, any_spec, any_spec, vspec, vspec, vspec] + [any_spec] * 5,
         out_specs=[any_spec, smem, any_spec, any_spec],
         scratch_shapes=[
             vm((n_tok, dim), BF16), vm((n_tok, dim), BF16), vm((n_tok, dim), BF16), vm((n_tok, ffn), BF16), vm((n_tok, ffn), BF16), vm((n_tok, dim), BF16),
-            vm((dim, n_tok), BF16), vm((dim, n_tok), BF16), vm((n_tok, dim), BF16), vm((plan.calc_rows, n_tok), BF16), vm((1, n_tok), F32),
+            vm((dim, n_tok), BF16), vm((dim, n_tok), BF16), vm((n_tok, dim), F32), vm((plan.calc_rows, n_tok), BF16), vm((1, n_tok), F32),
             vm((2, plan.calc_rows, dim), BF16), vm((2, plan.calc_rows, dim), F32), vm((3, plan.copy_rows, dim), F32),
             vm((2, dim, wblk), F32), vm((2, wblk, dim), F32),
             dma((6,)), dma((2,)), dma((3,)), dma((2, 2)), dma((3,)), dma((2,)), dma((2,)),
@@ -793,7 +859,7 @@
         compiler_params=pltpu.CompilerParams(vmem_limit_bytes=67_000_000),
         cost_estimate=pl.CostEstimate(flops=2 * n_tok * vocab * dim, bytes_accessed=5 * vocab * dim, transcendentals=0),
         name="fin",
-    )(cnt, emb, tmp, n_all, stats, labels.reshape(1, n_tok), rank, sid, dx0, xs, hid, da, g)
+    )(meta.reshape(-1), emb, tmp, n_all, stats, labels.reshape(1, n_tok), meta, dx0, xs, hid, da, g)
 
 
 def solution(mesh):
@@ -810,11 +876,11 @@
             for lo, rows in ((plan.calc_start(s), plan.calc_rows), (plan.copy_start(s), plan.copy_rows)):
                 cuts += [lo, lo + rows]
         cuts = jnp.array(cuts + [vocab] * (LANES - len(cuts)), jnp.int32).reshape(1, LANES)
-        x0, rank, sid, cnt = run_gather(tokens, emb, cuts, n_stage)
-        n_all, xs, hid, da, g, dx0, stats, tmp = run_pipe(x0, emb, w_up, w_down, labels, n_stage, plan)
+        x0 = run_gather(tokens, emb)
+        n_all, xs, hid, da, g, dx0, stats, tmp, meta = run_pipe(x0, emb, w_up, w_down, labels, tokens, cuts, n_stage, plan)
         flat = lambda p: p.reshape(n_tok, -1)
         grad_emb, loss, grad_up, grad_down = run_fin(
-            emb, tmp.reshape(-1, dim), flat(n_all), stats, labels, rank, sid, cnt.reshape(LANES), flat(dx0), flat(xs), flat(hid), flat(da), flat(g), n_stage, plan
+            emb, tmp.reshape(-1, dim), flat(n_all), stats, labels, meta, flat(dx0), flat(xs), flat(hid), flat(da), flat(g), n_stage, plan
         )
         return loss, grad_up[None], grad_down[None], grad_emb
 

time: 200 us -> 178 us (0.89)
  Pallas kernels: 195 us -> 175 us
  local copies, waits for them, and re-layouts: 3.73 us -> 0 us
    pallas_call x1, Pallas kernels: 128 us -> 116 us  [run_pipe(): pl.pallas_call(functools.partial(pipe_kernel, n_stage, plan), out_shape=[...]
    pallas_call x1, Pallas kernels: 63.2 us -> 55.6 us  [run_fin(): pl.pallas_call(functools.partial(fin_kernel, n_stage, n_tok, plan), out_s...]
    unnamed x12 -> x0, local copies, waits for them, and re-layouts: 3.73 us -> none
where the time goes in v3:
time: 178 us; the launch traced here: 176 us
  Pallas kernels  175 us (98%)
    pallas_call x1, Pallas kernels, run_pipe(): pl.pallas_call(functools.partial(pipe_kernel, n_stage, plan), out_shape=[...  116 us
    pallas_call x1, Pallas kernels, run_fin(): pl.pallas_call(functools.partial(fin_kernel, n_stage, n_tok, plan), out_s...  55.6 us
    pallas_call x1, Pallas kernels, run_gather(): pl.pallas_call(gather_kernel, out_shape=jax.ShapeDtypeStruct((2, seq, dim...  3.83 us

profile of v3, /device:TPU:125, one launch (start us, length us, event | category | flops | bytes accessed | tf_op | source)
XLA Modules:
  0.0 176.2 jit_solution(7312557797884398502)
XLA Ops:
  0.6 3.8 %gather.1.x0_hbm = bf16[2,128,512]{2,1,0:T(8,128)(2,1)} custom-call(s32[1024]{0:T(1024)} %bitcast.15, s32[8,128]{1,0:T(8,128)} %tok_ref.1, bf16[32128,512]{1,0:T(8,128)(2,1)} %emb_hbm.5), custom_call_target="tpu_custom_call" | custom-call | flops 1000000000 | bytes 4194304 | tf_op jit(solution)/shard_map/gather/pallas_call | solution.py:91
  4.5 115.9 %pipe.1 = (bf16[8,128,512]{2,1,0:T(8,128)(2,1)}, bf16[8,128,512]{2,1,0:T(8,128)(2,1)}, bf16[8,128,2048]{2,1,0:T(8,128)(2,1)}, bf16[8,128,2048]{2,1,0:T(8,128)(2,...) custom-call(bf16[2,128,512]{2,1,0:T(8,128)(2,1)} %gather.1.x0_hbm, ...), custom_call_target="tpu_custom_call" | custom-call | flops 60000002048 | bytes 100000000 | tf_op jit(solution)/shard_map/pipe/pallas_call | solution.py:640
  120.4 55.6 %fin.1 = (f32[32128,512]{1,0:T(8,128)}, f32[1]{0:T(128)}, f32[512,2048]{1,0:T(8,128)}, f32[2048,512]{1,0:T(8,128)}) custom-call(s32[3072]{0:T(1024)} %bitcast.30, bf16[32128,512]{1,0:T(8,128)(2,1)} %emb_hbm.5, f32[18432,512]{1,0:T(8,128)} %bitcast.21, bf16[1024,512]{1,0:T(8,128)(2,1)} %bitcast.26, f32[8,8,256]{2,1,0:T(8,128)} %get-tuple-element.20.stat_ref, ...), custom_call_target="tpu_custom_call" | custom-call | flops 33688649728 | bytes 82247680 | tf_op jit(solution)/shard_map/fin/pallas_call | solution.py:847
